TPU v7x, 32 devices: a whole 2x2x4 slice. The times are simulated.
32 devices in a mesh: rep: 2 (over y), dev: 4 (over z), col: 4 (over x, core).
Axes of the slice: x: 2, y: 2, z: 4, core: 2. Of those that a mesh axis runs over, the one named last changes fastest.
Arguments:
- queries: bfloat16 [256, 8192], P(('rep', 'dev'), 'col'), parts along dimension 0
- kv_pages: bfloat16 [768, 8, 2, 128, 128], P(('rep', 'dev'), 'col'), parts along dimension 0
- page_table: int32 [256, 3], P(('rep', 'dev')), parts along dimension 0, may hold values from 0 to 95, as said below
- seq_lengths: int32 [256], P(('rep', 'dev')), parts along dimension 0, may hold values from 2 to 384, as said below
- ffn_seat: int32 [256], P('rep'), parts along dimension 0, may hold values from 0 to 127, each once
- resid: bfloat16 [256, 8192], P(('rep', 'col'), 'dev'), parts along dimension 0, may hold values from -6 to 6
- w_out: bfloat16 [8192, 8192], P('col', 'dev'), may hold values from -0.0625 to 0.0625
- norm_gain: float32 [8192], P('dev'), may hold values from 0.25 to 1.75
- w_gate: bfloat16 [8192, 14336], P('dev', 'col'), may hold values from -0.0625 to 0.0625
- w_up: bfloat16 [8192, 14336], P('dev', 'col'), may hold values from -0.0625 to 0.0625
- w_down: bfloat16 [14336, 8192], P('col', 'dev'), may hold values from -0.046875 to 0.046875
Outputs:
- layer_out: bfloat16 [256, 8192], P(('rep', 'col'), 'dev'), parts along dimension 0
There are 2 independent parts, one for each index of `rep`. A program takes and returns all parts, laid end to end along the dimension named above; an argument that names none is the same for every part. Nothing has to cross between parts.
Inputs may be any that keep to these rules, and one draw needn't show every extreme that they name: `page_table`: the 32 rows of one dev index hold each block 0 to 95 of that index's pool exactly once. `seq_lengths`: the first sequence has 384 cached tokens.
All inputs are finite; a program needn't handle non-finite values.
Results may differ from a plain program's by a relative error of at most 0.017.
Values may be sent and summed in bfloat16 or wider, within the bound.
A program may use at most 128 MiB of HBM per device.

v0:
```python
import functools

import jax
import jax.numpy as jnp
from jax import lax
from jax.experimental import pallas as pl
from jax.experimental.pallas import tpu as pltpu
from jax.sharding import PartitionSpec as P

MESH = pl.DeviceIdType.MESH
F32 = jnp.float32
BF16 = jnp.bfloat16


def divisor(size, choices):
    for choice in choices:
        if size % choice == 0:
            return choice
    return size


def attend_kernel(seqs, pages, kv_local, table_ref, len_ref, q_ref, *refs):
    blocks, out_ref = refs[:-1], refs[-1]
    step = pl.program_id(0)
    page, head_dim = blocks[0].shape[3], blocks[0].shape[4]
    span = pages * page
    scale = head_dim ** (-0.5)
    for s in range(seqs):
        length = len_ref[step * seqs + s]
        for h in range(kv_local):
            query = q_ref[s, h]
            scores = jnp.concatenate(
                [
                    lax.dot_general(
                        query,
                        blocks[s * pages + j][0, h, 0],
                        (((1,), (1,)), ((), ())),
                        preferred_element_type=F32,
                    )
                    for j in range(pages)
                ],
                axis=1,
            ) * scale
            live = lax.broadcasted_iota(jnp.int32, scores.shape, 1) < length
            scores = jnp.where(live, scores, -1e30)
            top = jnp.max(scores, axis=1, keepdims=True)
            expo = jnp.exp(scores - top)
            weights = (expo / jnp.sum(expo, axis=1, keepdims=True)).astype(BF16)
            total = None
            for j in range(pages):
                part = jnp.dot(
                    weights[:, j * page : (j + 1) * page],
                    blocks[s * pages + j][0, h, 1],
                    preferred_element_type=F32,
                )
                total = part if total is None else total + part
            out_ref[s, h] = total.astype(BF16)


def attend(queries, kv_pages, page_table, seq_lengths):
    count = queries.shape[0]
    _, kv_local, _, page, head_dim = kv_pages.shape
    pages = page_table.shape[1]
    group = queries.shape[1] // (kv_local * head_dim)
    seqs = divisor(count, (4, 2, 1))

    def block_map(s, j, i, table, lens):
        return (table[(i * seqs + s) * pages + j], 0, 0, 0, 0)

    kv_specs = [
        pl.BlockSpec((1, kv_local, 2, page, head_dim), functools.partial(block_map, s, j))
        for s in range(seqs)
        for j in range(pages)
    ]
    q_spec = pl.BlockSpec((seqs, kv_local, group, head_dim), lambda i, table, lens: (i, 0, 0, 0))
    out = pl.pallas_call(
        functools.partial(attend_kernel, seqs, pages, kv_local),
        grid_spec=pltpu.PrefetchScalarGridSpec(
            num_scalar_prefetch=2,
            grid=(count // seqs,),
            in_specs=[q_spec] + kv_specs,
            out_specs=q_spec,
        ),
        out_shape=jax.ShapeDtypeStruct((count, kv_local, group, head_dim), BF16),
        compiler_params=pltpu.CompilerParams(dimension_semantics=("arbitrary",)),
    )(
        page_table.reshape(-1),
        seq_lengths,
        queries.reshape(count, kv_local, group, head_dim),
        *([kv_pages] * len(kv_specs)),
    )
    return out.reshape(count, -1)


def layer_kernel(
    nd,
    nc,
    dims,
    att_ref,
    seat_ref,
    resid_ref,
    gain_ref,
    wo_hbm,
    wg_hbm,
    wu_hbm,
    wd_hbm,
    out_ref,
    wo,
    wg,
    wu,
    wd,
    att_all,
    seated,
    proj,
    rs_in,
    x_all,
    ss_all,
    stream,
    own,
    in_r,
    in_l,
    ss_own,
    ss_r,
    ss_l,
    inv,
    hid,
    acc,
    down,
    down_in,
    w_sem,
    f_sem,
    att_s,
    att_r,
    rs_s,
    rs_r,
    x_s,
    x_r,
    ssc_s,
    ssc_r,
    sum_s,
    sum_r,
    ssd_s,
    ssd_r,
    hid_s,
    hid_r,
    dn_s,
    dn_r,
):
    T, B, R, HK, WC, NJ, AC, NA, CF, NC, half, full = dims
    me = lax.axis_index("dev")
    mc = lax.axis_index("col")
    E = nd - 1

    def peer_of(k):
        return lax.rem(mc + k, nc)

    def wo_copy(j):
        cols = pl.ds(pl.multiple_of(j * WC, WC), WC)
        return pltpu.make_async_copy(wo_hbm.at[:, cols], wo.at[j], w_sem.at[j])

    def ffn_copy(which, c):
        span = pl.ds(pl.multiple_of(c * CF, CF), CF)
        source = (wg_hbm.at[:, span], wu_hbm.at[:, span], wd_hbm.at[span, :])[which]
        return pltpu.make_async_copy(source, (wg, wu, wd)[which].at[c], f_sem.at[which, c])

    @pl.loop(0, NJ)
    def _(j):
        wo_copy(j).start()

    @pl.loop(0, NC)
    def _(c):
        ffn_copy(0, c).start()
        ffn_copy(1, c).start()

    @pl.loop(0, NC)
    def _(c):
        ffn_copy(2, c).start()

    barrier = pltpu.get_barrier_semaphore()

    @pl.when(me > 0)
    def _():
        pl.semaphore_signal(barrier, inc=1, device_id={"dev": me - 1}, device_id_type=MESH)

    @pl.when(me < E)
    def _():
        pl.semaphore_signal(barrier, inc=1, device_id={"dev": me + 1}, device_id_type=MESH)

    for k in range(1, nc):
        pl.semaphore_signal(barrier, inc=1, device_id={"col": peer_of(k)}, device_id_type=MESH)

    neighbours = jnp.where(me > 0, 1, 0) + jnp.where(me < E, 1, 0)
    pl.semaphore_wait(barrier, neighbours + (nc - 1))

    def att_rows(origin):
        return pl.ds(pl.multiple_of(origin * B, B), B)

    def att_copy(origin, a, way, from_input):
        cols = slice(a * AC, (a + 1) * AC)
        dst = att_all.at[att_rows(origin), cols]
        return pltpu.make_async_remote_copy(
            src_ref=att_ref.at[:, cols] if from_input else dst,
            dst_ref=dst,
            send_sem=att_s.at[way, origin, a],
            recv_sem=att_r.at[origin, a],
            device_id={"dev": me + (1 if way == 0 else -1)},
            device_id_type=MESH,
        )

    for a in range(NA):
        @pl.when(me < E)
        def _():
            att_copy(me, a, 0, True).start()

        @pl.when(me > 0)
        def _():
            att_copy(me, a, 1, True).start()

    att_all[att_rows(me), :] = att_ref[...]

    @pl.loop(1, nd)
    def _(k):
        for a in range(NA):
            @pl.when(me - k >= 0)
            def _():
                att_copy(me - k, a, 0, False).wait_recv()

                @pl.when(me < E)
                def _():
                    att_copy(me - k, a, 0, False).start()

            @pl.when(me + k <= E)
            def _():
                att_copy(me + k, a, 1, False).wait_recv()

                @pl.when(me > 0)
                def _():
                    att_copy(me + k, a, 1, False).start()

    pick = (lax.broadcasted_iota(jnp.int32, (T, T), 0) == seat_ref[...]).astype(F32).astype(BF16)
    seated[...] = jnp.dot(pick, att_all[...], preferred_element_type=F32).astype(BF16)

    def rs_copy(k, j, source, target, send, recv):
        cols = pl.ds(pl.multiple_of(j * WC, WC), WC)
        rows = pl.ds(pl.multiple_of(peer_of(k) * R, R), R)
        return pltpu.make_async_remote_copy(
            src_ref=source.at[rows, cols],
            dst_ref=target.at[k - 1, :, cols],
            send_sem=send.at[k - 1, j],
            recv_sem=recv.at[k - 1, j],
            device_id={"col": peer_of(k)},
            device_id_type=MESH,
        )

    @pl.loop(0, NJ)
    def _(j):
        wo_copy(j).wait()
        cols = pl.ds(pl.multiple_of(j * WC, WC), WC)
        proj[:, cols] = jnp.dot(seated[...], wo[j], preferred_element_type=F32).astype(BF16)
        for k in range(1, nc):
            rs_copy(k, j, proj, rs_in, rs_s, rs_r).start()

    my_rows = pl.ds(pl.multiple_of(mc * R, R), R)

    def x_copy(k, j):
        spot = x_all.at[my_rows, pl.ds(pl.multiple_of(j * WC, WC), WC)]
        return pltpu.make_async_remote_copy(
            src_ref=spot,
            dst_ref=spot,
            send_sem=x_s.at[k - 1, j],
            recv_sem=x_r.at[k - 1, j],
            device_id={"col": peer_of(k)},
            device_id_type=MESH,
        )

    def ssc_copy(k):
        spot = ss_all.at[my_rows, :]
        return pltpu.make_async_remote_copy(
            src_ref=spot,
            dst_ref=spot,
            send_sem=ssc_s.at[k - 1],
            recv_sem=ssc_r.at[k - 1],
            device_id={"col": peer_of(k)},
            device_id_type=MESH,
        )

    squares = jnp.zeros((R, 1), F32)
    for j in range(NJ):
        cols = slice(j * WC, (j + 1) * WC)
        value = resid_ref[:, cols].astype(F32) + proj[my_rows, cols].astype(F32)
        for k in range(1, nc):
            rs_copy(k, j, proj, rs_in, rs_s, rs_r).wait_recv()
            value = value + rs_in[k - 1, :, cols].astype(F32)
        stream[:, cols] = value
        squares = squares + jnp.sum(value * value, axis=1, keepdims=True)
        x_all[my_rows, cols] = (value * gain_ref[:, cols]).astype(BF16)
        for k in range(1, nc):
            x_copy(k, j).start()
    ss_all[my_rows, :] = jnp.broadcast_to(squares, (R, ss_all.shape[1]))
    for k in range(1, nc):
        ssc_copy(k).start()
    for k in range(1, nc):
        for j in range(NJ):
            x_copy(k, j).wait_recv()
        ssc_copy(k).wait_recv()
    ss_own[...] = ss_all[...]

    def neighbour(way):
        return {"dev": me + (1 if way == 0 else -1)}

    def sum_copy(way, c):
        return pltpu.make_async_remote_copy(
            src_ref=own.at[c, 1 - way],
            dst_ref=(in_r if way == 0 else in_l).at[c],
            send_sem=sum_s.at[way, c],
            recv_sem=sum_r.at[way, c],
            device_id=neighbour(way),
            device_id_type=MESH,
        )

    def ssd_copy(way):
        return pltpu.make_async_remote_copy(
            src_ref=ss_own.at[pl.ds((1 - way) * half, half), :],
            dst_ref=ss_r if way == 0 else ss_l,
            send_sem=ssd_s.at[way],
            recv_sem=ssd_r.at[way],
            device_id=neighbour(way),
            device_id_type=MESH,
        )

    def hid_copy(way, c):
        spot = hid.at[c, pl.ds(way * half, half), :]
        return pltpu.make_async_remote_copy(
            src_ref=spot,
            dst_ref=spot,
            send_sem=hid_s.at[way, c],
            recv_sem=hid_r.at[way, c],
            device_id=neighbour(way),
            device_id_type=MESH,
        )

    def sum_stage(way, c):
        first = 0 if way == 0 else E
        last = E - first
        part = 1 - way
        incoming = in_r if way == 0 else in_l
        ss_in = ss_r if way == 0 else ss_l
        ss_rows = pl.ds(part * half, half)

        @pl.when(c == 0)
        def _():
            @pl.when(me != first)
            def _():
                ssd_copy(way).wait_recv()
                ss_own[ss_rows, :] = ss_own[ss_rows, :] + ss_in[...]

            @pl.when(me != last)
            def _():
                ssd_copy(way).start()

            @pl.when(me == last)
            def _():
                inv[...] = lax.rsqrt(ss_own[ss_rows, :] / full + 1e-5)

        @pl.when(me != first)
        def _():
            sum_copy(way, c).wait_recv()

            @pl.when(me != last)
            def _():
                total = own[c, part].astype(F32) + incoming[c].astype(F32)
                own[c, part] = total.astype(BF16)

        @pl.when(me != last)
        def _():
            sum_copy(way, c).start()

        @pl.when(me == last)
        def _():
            total = own[c, part].astype(F32) + incoming[c].astype(F32)
            scale = inv[:, 0:1]
            gate = total[:, :CF] * scale
            up = total[:, CF:] * scale
            hid[c, part * half : (part + 1) * half, :] = (
                gate / (1.0 + jnp.exp(-gate)) * up
            ).astype(BF16)
            hid_copy(part, c).start()

    def hid_stage(way, c):
        first = 0 if way == 0 else E
        last = E - first

        @pl.when(me != first)
        def _():
            hid_copy(way, c).wait_recv()

            @pl.when(me != last)
            def _():
                hid_copy(way, c).start()

    def inside(c):
        return jnp.logical_and(c >= 0, c < NC)

    acc[...] = jnp.zeros_like(acc)

    @pl.loop(0, NC + 2 * E)
    def _(i):
        @pl.when(i < NC)
        def _():
            ffn_copy(0, i).wait()
            gate = jnp.dot(x_all[...], wg[i], preferred_element_type=F32).astype(BF16)
            own[i, 0, :, :CF] = gate[:half]
            own[i, 1, :, :CF] = gate[half:]
            ffn_copy(1, i).wait()
            up = jnp.dot(x_all[...], wu[i], preferred_element_type=F32).astype(BF16)
            own[i, 0, :, CF:] = up[:half]
            own[i, 1, :, CF:] = up[half:]

        for way in (0, 1):
            c = i - (me if way == 0 else E - me)

            @pl.when(inside(c))
            def _():
                sum_stage(way, c)

        for way in (0, 1):
            c = i - E - (me if way == 0 else E - me)

            @pl.when(inside(c))
            def _():
                hid_stage(way, c)

        c = i - E - jnp.maximum(me, E - me)

        @pl.when(inside(c))
        def _():
            ffn_copy(2, c).wait()
            for j in range(NJ):
                cols = slice(j * WC, (j + 1) * WC)
                acc[:, cols] += jnp.dot(hid[c], wd[c, :, cols], preferred_element_type=F32)

    for j in range(NJ):
        cols = slice(j * WC, (j + 1) * WC)
        down[:, cols] = acc[:, cols].astype(BF16)
        for k in range(1, nc):
            rs_copy(k, j, down, down_in, dn_s, dn_r).start()
    for j in range(NJ):
        cols = slice(j * WC, (j + 1) * WC)
        value = stream[:, cols] + acc[my_rows, cols]
        for k in range(1, nc):
            rs_copy(k, j, down, down_in, dn_s, dn_r).wait_recv()
            value = value + down_in[k - 1, :, cols].astype(F32)
        out_ref[:, cols] = value.astype(BF16)

    for k in range(1, nc):
        for j in range(NJ):
            rs_copy(k, j, proj, rs_in, rs_s, rs_r).wait_send()
            x_copy(k, j).wait_send()
            rs_copy(k, j, down, down_in, dn_s, dn_r).wait_send()
        ssc_copy(k).wait_send()

    for a in range(NA):
        @pl.loop(0, nd)
        def _(origin):
            @pl.when(jnp.logical_and(me < E, origin <= me))
            def _():
                att_copy(origin, a, 0, False).wait_send()

            @pl.when(jnp.logical_and(me > 0, origin >= me))
            def _():
                att_copy(origin, a, 1, False).wait_send()

    for way in (0, 1):
        @pl.when(me != (E if way == 0 else 0))
        def _():
            ssd_copy(way).wait_send()

            @pl.loop(0, NC)
            def _(c):
                sum_copy(way, c).wait_send()
                hid_copy(way, c).wait_send()


def layer(nd, nc, attended, seats, resid, gain, w_out, w_gate, w_up, w_down):
    B, HK = attended.shape
    T = seats.shape[1]
    R, DK = resid.shape
    FK = w_gate.shape[1]
    WC = divisor(DK, (1024, 512, 256, 128))
    NJ = DK // WC
    AC = divisor(HK, (1024, 512, 256, 128))
    NA = HK // AC
    CF = divisor(FK, (896, 512, 256, 128))
    NC = FK // CF
    half = T // 2
    dims = (T, B, R, HK, WC, NJ, AC, NA, CF, NC, half, float(DK * nd))
    dma = pltpu.SemaphoreType.DMA
    vmem = pl.BlockSpec(memory_space=pltpu.VMEM)
    hbm = pl.BlockSpec(memory_space=pltpu.HBM)
    scratch = [
        pltpu.VMEM((NJ, HK, WC), BF16),
        pltpu.VMEM((NC, DK, CF), BF16),
        pltpu.VMEM((NC, DK, CF), BF16),
        pltpu.VMEM((NC, CF, DK), BF16),
        pltpu.VMEM((T, HK), BF16),
        pltpu.VMEM((T, HK), BF16),
        pltpu.VMEM((T, DK), BF16),
        pltpu.VMEM((nc - 1, R, DK), BF16),
        pltpu.VMEM((T, DK), BF16),
        pltpu.VMEM((T, 128), F32),
        pltpu.VMEM((R, DK), F32),
        pltpu.VMEM((NC, 2, half, 2 * CF), BF16),
        pltpu.VMEM((NC, half, 2 * CF), BF16),
        pltpu.VMEM((NC, half, 2 * CF), BF16),
        pltpu.VMEM((T, 128), F32),
        pltpu.VMEM((half, 128), F32),
        pltpu.VMEM((half, 128), F32),
        pltpu.VMEM((half, 128), F32),
        pltpu.VMEM((NC, T, CF), BF16),
        pltpu.VMEM((T, DK), F32),
        pltpu.VMEM((T, DK), BF16),
        pltpu.VMEM((nc - 1, R, DK), BF16),
        dma((NJ,)),
        dma((3, NC)),
        dma((2, nd, NA)),
        dma((nd, NA)),
        dma((nc - 1, NJ)),
        dma((nc - 1, NJ)),
        dma((nc - 1, NJ)),
        dma((nc - 1, NJ)),
        dma((nc - 1,)),
        dma((nc - 1,)),
        dma((2, NC)),
        dma((2, NC)),
        dma((2,)),
        dma((2,)),
        dma((2, NC)),
        dma((2, NC)),
        dma((nc - 1, NJ)),
        dma((nc - 1, NJ)),
    ]
    return pl.pallas_call(
        functools.partial(layer_kernel, nd, nc, dims),
        out_shape=jax.ShapeDtypeStruct((R, DK), BF16),
        in_specs=[vmem] * 4 + [hbm] * 4,
        out_specs=vmem,
        scratch_shapes=scratch,
        compiler_params=pltpu.CompilerParams(
            collective_id=0, has_side_effects=True, vmem_limit_bytes=67043328
        ),
    )(attended, seats, resid, gain, w_out, w_gate, w_up, w_down)


def solution(mesh):
    nd, nc = mesh.shape["dev"], mesh.shape["col"]

    def on_device(
        queries,
        kv_pages,
        page_table,
        seq_lengths,
        ffn_seat,
        resid,
        w_out,
        norm_gain,
        w_gate,
        w_up,
        w_down,
    ):
        attended = attend(queries, kv_pages, page_table, seq_lengths)
        return layer(
            nd, nc, attended, ffn_seat[None, :], resid, norm_gain[None, :], w_out, w_gate, w_up, w_down
        )

    in_specs = (
        P(("rep", "dev"), "col"),
        P(("rep", "dev"), "col", None, None, None),
        P(("rep", "dev"), None),
        P(("rep", "dev")),
        P("rep"),
        P(("rep", "col"), "dev"),
        P("col", "dev"),
        P("dev"),
        P("dev", "col"),
        P("dev", "col"),
        P("col", "dev"),
    )
    return jax.shard_map(
        on_device,
        mesh=mesh,
        in_specs=in_specs,
        out_specs=P(("rep", "col"), "dev"),
        check_vma=False,
    )
```

profile of v0, /device:TPU:0, one launch (start us, length us, event | category | flops | bytes accessed | tf_op | source)
XLA Modules:
  0.0 121.7 jit_solution(952234553524329088)
XLA Ops:
  0.0 0.8 copy.13
  0.8 0.6 reshape.9.table_ref
  1.4 1.6 %copy.14 = bf16[4,8,16,128]{3,2,1,0:T(8,128)(2,1)} copy(bf16[4,8,16,128]{3,1,2,0:T(8,128)(2,1)} %bitcast.13) | data formatting | bytes 262144
  3.0 27.5 %shard_map.109 = bf16[32,2,8,128]{3,2,1,0:T(8,128)(2,1)} custom-call(s32[96]{0:T(128)} %reshape.9.table_ref, s32[32]{0:T(128)} %len_ref.1, bf16[32,2,8,128]{3,2,1,0:T(8,128)(2,1)} %bitcast.12, bf16[96,2,2,128,128]{4,3,2,1,0:T(8,128)(2,1)} %refs_11_.1, bf16[96,2,2,128,128]{4,3,2,1,0:T(8,128)(2,1)} %refs_11_.1, bf16[96,2,2,128,128]{4,3,2,1,0:T(8,128)(2,1)} %refs_11_.1, ...), custom_call_target="tpu_custom_call" | custom-call | tf_op jit(solution)/shard_map/pallas_call | solution.py:76
  30.5 1.6 %copy.17 = bf16[4,8,16,128]{3,1,2,0:T(8,128)(2,1)} copy(bf16[4,8,16,128]{3,2,1,0:T(8,128)(2,1)} %bitcast.11) | data formatting | bytes 262144
  32.1 88.0 %shard_map.110 = bf16[32,2048]{1,0:T(8,128)(2,1)} custom-call(bf16[32,2048]{1,0:T(8,128)(2,1)} %bitcast.10, s32[1,128]{1,0:T(1,128)} %bitcast.15, bf16[32,2048]{1,0:T(8,128)(2,1)} %resid_ref.1, f32[1,2048]{1,0:T(1,128)} %bitcast.14, bf16[2048,2048]{1,0:T(8,128)(2,1)} %wo_hbm.1, bf16[2048,3584]{1,0:T(8,128)(2,1)} %wg_hbm.1, bf16[2048,3584]{1,0:T(8,128)(2,1)} %wu_hbm.1, ...), custom_call_target="tpu_custom_call" | custom-call | tf_op jit(solution)/shard_map/pallas_call | solution.py:542
  120.1 1.6 %copy.19 = bf16[32,2048]{1,0:T(8,128)(2,1)} copy(bf16[32,2048]{1,0:T(8,128)(2,1)} %shard_map.110) | data formatting | bytes 262144
where the time goes:
time: 122 us
  Pallas kernels  116 us (95%)
  local copies, waits for them, and re-layouts  6.11 us (5%)
    pallas_call x1, Pallas kernels, layer(): pl.pallas_call(functools.partial(layer_kernel, nd, nc, dims), out_shape=j...  88 us
    pallas_call x1, Pallas kernels, attend(): pl.pallas_call(functools.partial(attend_kernel, seqs, pages, kv_local), g...  27.5 us
    unnamed x4, local copies, waits for them, and re-layouts  5.5 us

commit v1 on v0

v1 whole, which is shorter than its diff:
```python
import functools

import jax
import jax.numpy as jnp
from jax import lax
from jax.experimental import pallas as pl
from jax.experimental.pallas import tpu as pltpu
from jax.sharding import PartitionSpec as P

MESH = pl.DeviceIdType.MESH
F32 = jnp.float32
BF16 = jnp.bfloat16
TILE = 128
SUB = 8


def divisor(size, choices):
    for choice in choices:
        if size % choice == 0:
            return choice
    return size


def layer_kernel(
    nd,
    nc,
    dims,
    table_hbm,
    len_hbm,
    q_hbm,
    kv_hbm,
    seat_hbm,
    resid_hbm,
    gain_hbm,
    wo_hbm,
    wg_hbm,
    wu_hbm,
    wd_hbm,
    out_hbm,
    table,
    lens,
    q_in,
    seat,
    resid,
    gain,
    wo,
    wg,
    wu,
    kpool,
    vpool,
    q_rows,
    o_rows,
    scores,
    att_all,
    seated,
    proj,
    rs_one,
    rs_mid,
    rs_two,
    x_all,
    stream,
    own,
    in_r,
    in_l,
    ss_own,
    ss_r,
    ss_l,
    inv,
    hid,
    acc,
    down,
    dn_one,
    dn_mid,
    dn_two,
    out,
    in_sem,
    kv_sem,
    w_sem,
    att_s,
    att_r,
    one_s,
    one_r,
    two_s,
    two_r,
    x_s,
    x_r,
    pair_s,
    pair_r,
    sum_s,
    sum_r,
    ssd_s,
    ssd_r,
    hid_s,
    hid_r,
    done_s,
    done_r,
    dtwo_s,
    dtwo_r,
):
    T, B, R, HK, DK, FK, kvl, group, pages, blocks, WC, NJ, CF, NC, half, NX, full = dims
    me = lax.axis_index("dev")
    mc = lax.axis_index("col")
    mx, core = mc // 2, mc % 2
    E = nd - 1
    heads = kvl * group
    span = pages * TILE
    KB = DK // TILE
    FB = FK // TILE
    KH = (KB + 1) // 2
    partner = {"col": mx * 2 + 1 - core}

    def x_peer(k):
        return lax.rem(mx + k, NX)

    def x_from(k):
        return lax.rem(mx + NX - k, NX)

    small = [
        pltpu.make_async_copy(table_hbm, table, in_sem.at[0]),
        pltpu.make_async_copy(len_hbm, lens, in_sem.at[1]),
        pltpu.make_async_copy(q_hbm, q_in, in_sem.at[2]),
        pltpu.make_async_copy(seat_hbm, seat, in_sem.at[3]),
        pltpu.make_async_copy(resid_hbm, resid, in_sem.at[4]),
        pltpu.make_async_copy(gain_hbm, gain, in_sem.at[5]),
    ]
    kv_count = blocks * kvl
    kv_copies = [
        pltpu.make_async_copy(
            kv_hbm.at[:, v], (kpool, vpool)[v].at[pl.ds(0, kv_count)], kv_sem.at[v]
        )
        for v in (0, 1)
    ]
    w_copies = [
        pltpu.make_async_copy(wo_hbm, wo, w_sem.at[0]),
        pltpu.make_async_copy(wg_hbm, wg, w_sem.at[1]),
        pltpu.make_async_copy(wu_hbm, wu, w_sem.at[2]),
    ]

    def wd_copy(n):
        cols = slice(n * TILE, (n + 1) * TILE)
        return pltpu.make_async_copy(
            wd_hbm.at[:, :, cols],
            (kpool, vpool)[n // KH].at[pl.ds(n % KH * FB, FB)],
            w_sem.at[3 + n],
        )

    for copy in small[:3]:
        copy.start()
    for copy in kv_copies:
        copy.start()
    for copy in small[3:]:
        copy.start()

    barrier = pltpu.get_barrier_semaphore()

    @pl.when(me > 0)
    def _():
        pl.semaphore_signal(barrier, inc=1, device_id={"dev": me - 1}, device_id_type=MESH)

    @pl.when(me < E)
    def _():
        pl.semaphore_signal(barrier, inc=1, device_id={"dev": me + 1}, device_id_type=MESH)

    for k in range(1, NX):
        pl.semaphore_signal(
            barrier, inc=1, device_id={"col": x_peer(k) * 2 + core}, device_id_type=MESH
        )
    pl.semaphore_signal(barrier, inc=1, device_id=partner, device_id_type=MESH)

    small[2].wait()
    for n in range(heads):
        q_rows[pl.ds(n, B, stride=heads), :] = q_in[:, n * TILE : (n + 1) * TILE].astype(F32)
    small[0].wait()
    small[1].wait()
    kv_copies[0].wait()
    w_copies[0].start()

    neighbours = jnp.where(me > 0, 1, 0) + jnp.where(me < E, 1, 0)

    PB = B // 2
    scale = TILE ** (-0.5)
    head_row = lax.broadcasted_iota(jnp.int32, (heads, TILE), 0) // group

    def blocked(value):
        if kvl == 1:
            return value.astype(BF16)
        wide = lax.broadcasted_iota(jnp.int32, value.shape, 0) // group
        return jnp.concatenate(
            [jnp.where(wide == h, value, 0.0).astype(BF16) for h in range(kvl)], axis=1
        )

    def att_copy(origin, a, way):
        spot = att_all.at[pl.ds(pl.multiple_of(origin * B + a * PB, PB), PB), :]
        return pltpu.make_async_remote_copy(
            src_ref=spot,
            dst_ref=spot,
            send_sem=att_s.at[way, origin, a],
            recv_sem=att_r.at[origin, a],
            device_id={"dev": me + (1 if way == 0 else -1)},
            device_id_type=MESH,
        )

    for a in range(2):
        @pl.loop(0, PB // SUB)
        def _(b):
            for u in range(SUB):
                spot = b * SUB + u
                s = a * PB + spot
                rows = pl.ds(pl.multiple_of(s * heads, heads), heads)
                query = blocked(q_rows[rows, :])
                keys = []
                for j in range(pages):
                    block = table[j, s]
                    keys.append(
                        jnp.concatenate([kpool[block * kvl + h] for h in range(kvl)], axis=1)
                        if kvl > 1
                        else kpool[block]
                    )
                value = lax.dot_general(
                    query,
                    jnp.concatenate(keys, axis=0),
                    (((1,), (1,)), ((), ())),
                    preferred_element_type=F32,
                ) * scale
                live = lax.broadcasted_iota(jnp.int32, value.shape, 1) < lens[s]
                scores[pl.ds(pl.multiple_of(spot * heads, heads), heads), :] = jnp.where(
                    live, value, -1e30
                )

        if a == 0:
            kv_copies[1].wait()
            w_copies[1].start()
            w_copies[2].start()

        @pl.loop(0, PB // SUB)
        def _(b):
            rows = pl.ds(pl.multiple_of(b * (SUB * heads), SUB * heads), SUB * heads)
            value = scores[rows, :]
            expo = jnp.exp(value - jnp.max(value, axis=1, keepdims=True))
            scores[rows, :] = expo / jnp.sum(expo, axis=1, keepdims=True)
            for u in range(SUB):
                spot = b * SUB + u
                s = a * PB + spot
                weights = blocked(
                    scores[pl.ds(pl.multiple_of(spot * heads, heads), heads), :]
                )
                vals = [
                    vpool[table[j, s] * kvl + h]
                    for h in range(kvl)
                    for j in range(pages)
                ]
                o_rows[pl.ds(pl.multiple_of(spot * heads, heads), heads), :] = jnp.dot(
                    weights, jnp.concatenate(vals, axis=0), preferred_element_type=F32
                )

        mine = pl.ds(pl.multiple_of(me * B + a * PB, PB), PB)
        for n in range(heads):
            att_all[mine, n * TILE : (n + 1) * TILE] = o_rows[
                pl.ds(n, PB, stride=heads), :
            ].astype(BF16)

        if a == 0:
            pl.semaphore_wait(barrier, neighbours + NX)

        @pl.when(me < E)
        def _():
            att_copy(me, a, 0).start()

        @pl.when(me > 0)
        def _():
            att_copy(me, a, 1).start()

    for n in range(KB):
        wd_copy(n).start()

    for copy in small[3:]:
        copy.wait()

    @pl.loop(1, nd)
    def _(k):
        for a in range(2):
            @pl.when(me - k >= 0)
            def _():
                att_copy(me - k, a, 0).wait_recv()

                @pl.when(me < E)
                def _():
                    att_copy(me - k, a, 0).start()

            @pl.when(me + k <= E)
            def _():
                att_copy(me + k, a, 1).wait_recv()

                @pl.when(me > 0)
                def _():
                    att_copy(me + k, a, 1).start()

    place = lax.broadcasted_iota(jnp.int32, (T, T), 0)
    position = place // R
    seat_here = ((position % NX) * 2 + position // NX) * R + place % R
    pick = (seat_here == seat[...]).astype(F32).astype(BF16)
    seated[...] = jnp.dot(pick, att_all[...], preferred_element_type=F32).astype(BF16)

    half_rows = NX * R
    my_half = pl.ds(pl.multiple_of(core * half_rows, half_rows), half_rows)
    other_half = pl.ds(pl.multiple_of((1 - core) * half_rows, half_rows), half_rows)

    def block_rows(c, x):
        return pl.ds(pl.multiple_of((c * NX + x) * R, R), R)

    my_rows = block_rows(core, mx)
    mid_own = pl.ds(pl.multiple_of(mx * R, R), R)

    def one_copy(j, source, target, send, recv):
        cols = slice(j * WC, (j + 1) * WC)
        return pltpu.make_async_remote_copy(
            src_ref=source.at[other_half, cols],
            dst_ref=target.at[:, cols],
            send_sem=send.at[j],
            recv_sem=recv.at[j],
            device_id=partner,
            device_id_type=MESH,
        )

    def two_copy(k, j, source, target, send, recv):
        cols = slice(j * WC, (j + 1) * WC)
        rows = pl.ds(pl.multiple_of(x_peer(k) * R, R), R)
        return pltpu.make_async_remote_copy(
            src_ref=source.at[rows, cols],
            dst_ref=target.at[k - 1, :, cols],
            send_sem=send.at[k - 1, j],
            recv_sem=recv.at[k - 1, j],
            device_id={"col": x_peer(k) * 2 + core},
            device_id_type=MESH,
        )

    one_args = (proj, rs_one, one_s, one_r)
    two_args = (rs_mid, rs_two, two_s, two_r)
    done_args = (down, dn_one, done_s, done_r)
    dtwo_args = (dn_mid, dn_two, dtwo_s, dtwo_r)

    def meet(j, source, arrived, middle, one, two):
        cols = slice(j * WC, (j + 1) * WC)
        one_copy(j, *one).wait_recv()
        middle[:, cols] = (
            source[my_half, cols].astype(F32) + arrived[:, cols].astype(F32)
        ).astype(BF16)
        for k in range(1, NX):
            two_copy(k, j, *two).start()

    w_copies[0].wait()
    for j in range(NJ + 1):
        if j < NJ:
            cols = slice(j * WC, (j + 1) * WC)
            proj[:, cols] = jnp.dot(
                seated[...], wo[:, cols], preferred_element_type=F32
            ).astype(BF16)
            one_copy(j, *one_args).start()
        if j > 0:
            meet(j - 1, proj, rs_one, rs_mid, one_args, two_args)

    def x_copy(k, j):
        spot = x_all.at[my_rows, j * WC : (j + 1) * WC]
        return pltpu.make_async_remote_copy(
            src_ref=spot,
            dst_ref=spot,
            send_sem=x_s.at[k - 1, j],
            recv_sem=x_r.at[k - 1, j],
            device_id={"col": x_peer(k) * 2 + core},
            device_id_type=MESH,
        )

    def pair_copy(k, j):
        spot = x_all.at[block_rows(core, x_from(k)), j * WC : (j + 1) * WC]
        return pltpu.make_async_remote_copy(
            src_ref=spot,
            dst_ref=spot,
            send_sem=pair_s.at[k, j],
            recv_sem=pair_r.at[k, j],
            device_id=partner,
            device_id_type=MESH,
        )

    for j in range(NJ):
        cols = slice(j * WC, (j + 1) * WC)
        value = (
            resid[:, cols].astype(F32)
            + proj[my_rows, cols].astype(F32)
            + rs_one[mid_own, cols].astype(F32)
        )
        for k in range(1, NX):
            two_copy(k, j, *two_args).wait_recv()
            value = value + rs_two[k - 1, :, cols].astype(F32)
        stream[:, cols] = value
        x_all[my_rows, cols] = (value * gain[:, cols]).astype(BF16)
        for k in range(1, NX):
            x_copy(k, j).start()
        pair_copy(0, j).start()
    for j in range(NJ):
        for k in range(1, NX):
            x_copy(k, j).wait_recv()
            pair_copy(k, j).start()
    for j in range(NJ):
        for k in range(NX):
            pair_copy(k, j).wait_recv()

    def neighbour(way):
        return {"dev": me + (1 if way == 0 else -1)}

    def sum_copy(way, c):
        return pltpu.make_async_remote_copy(
            src_ref=own.at[c, 1 - way],
            dst_ref=(in_r if way == 0 else in_l).at[c],
            send_sem=sum_s.at[way, c],
            recv_sem=sum_r.at[way, c],
            device_id=neighbour(way),
            device_id_type=MESH,
        )

    def ssd_copy(way):
        return pltpu.make_async_remote_copy(
            src_ref=ss_own.at[pl.ds((1 - way) * half, half), :],
            dst_ref=ss_r if way == 0 else ss_l,
            send_sem=ssd_s.at[way],
            recv_sem=ssd_r.at[way],
            device_id=neighbour(way),
            device_id_type=MESH,
        )

    def hid_copy(way, c):
        spot = hid.at[c, pl.ds(way * half, half), :]
        return pltpu.make_async_remote_copy(
            src_ref=spot,
            dst_ref=spot,
            send_sem=hid_s.at[way, c],
            recv_sem=hid_r.at[way, c],
            device_id=neighbour(way),
            device_id_type=MESH,
        )

    def sum_stage(way, c):
        first = 0 if way == 0 else E
        last = E - first
        part = 1 - way
        incoming = in_r if way == 0 else in_l
        ss_in = ss_r if way == 0 else ss_l
        ss_rows = pl.ds(part * half, half)

        @pl.when(c == 0)
        def _():
            ssd_copy(way).wait_recv()
            ss_own[ss_rows, :] = ss_own[ss_rows, :] + ss_in[...]

            @pl.when(me != last)
            def _():
                ssd_copy(way).start()

            @pl.when(me == last)
            def _():
                inv[...] = lax.rsqrt(ss_own[ss_rows, :] / full + 1e-5)

        sum_copy(way, c).wait_recv()

        @pl.when(me != last)
        def _():
            total = own[c, part].astype(F32) + incoming[c].astype(F32)
            own[c, part] = total.astype(BF16)
            sum_copy(way, c).start()

        @pl.when(me == last)
        def _():
            total = own[c, part].astype(F32) + incoming[c].astype(F32)
            factor = inv[:, 0:1]
            gate = total[:, :CF] * factor
            up = total[:, CF:] * factor
            hid[c, part * half : (part + 1) * half, :] = (
                gate / (1.0 + jnp.exp(-gate)) * up
            ).astype(BF16)
            hid_copy(part, c).start()

    def hid_stage(way, c):
        last = E if way == 0 else 0
        hid_copy(way, c).wait_recv()

        @pl.when(me != last)
        def _():
            hid_copy(way, c).start()

    def inside(c):
        return jnp.logical_and(c >= 0, c < NC)

    PACE = 2

    def sum_lag(d):
        return (5 * d + 1) // 2

    first_hid = max(NC + 2, (5 * E + 1) // 2 + 1)

    def hid_lag(d):
        return first_hid + (5 * (d - 1)) // 2

    acc[...] = jnp.zeros_like(acc)
    w_copies[1].wait()
    w_copies[2].wait()

    @pl.loop(0, NC + first_hid + (5 * (E - 1)) // 2)
    def _(i):
        for p in range(PACE):
            q = i * PACE + p

            @pl.when(q < NC)
            def _():
                cols = pl.ds(pl.multiple_of(q * CF, CF), CF)
                gate = jnp.dot(x_all[...], wg[:, cols], preferred_element_type=F32).astype(BF16)
                own[q, 0, :, :CF] = gate[:half]
                own[q, 1, :, :CF] = gate[half:]
                up = jnp.dot(x_all[...], wu[:, cols], preferred_element_type=F32).astype(BF16)
                own[q, 0, :, CF:] = up[:half]
                own[q, 1, :, CF:] = up[half:]
                for way in (0, 1):
                    @pl.when(me == (0 if way == 0 else E))
                    def _():
                        sum_copy(way, q).start()

        @pl.when(i == 0)
        def _():
            squares = jnp.zeros((T, 1), F32)
            for j in range(NJ):
                cols = slice(j * WC, (j + 1) * WC)
                value = x_all[:, cols].astype(F32) / gain[:, cols]
                squares = squares + jnp.sum(value * value, axis=1, keepdims=True)
            ss_own[...] = jnp.broadcast_to(squares, (T, ss_own.shape[1]))
            for way in (0, 1):
                @pl.when(me == (0 if way == 0 else E))
                def _():
                    ssd_copy(way).start()

        for way in (0, 1):
            d = me if way == 0 else E - me
            c = i - sum_lag(d)

            @pl.when(jnp.logical_and(d > 0, inside(c)))
            def _():
                sum_stage(way, c)

        for way in (0, 1):
            d = me if way == 0 else E - me
            c = i - hid_lag(d)

            @pl.when(jnp.logical_and(d > 0, inside(c)))
            def _():
                hid_stage(way, c)

        c = i - hid_lag(jnp.maximum(me, E - me))

        @pl.when(i == hid_lag(jnp.maximum(me, E - me)))
        def _():
            for n in range(KB):
                wd_copy(n).wait()

        @pl.when(inside(c))
        def _():
            per = CF // TILE
            wide = 2 if KB % 2 == 0 else 1
            value = hid[c]
            for n in range(0, KB, wide):
                right = [
                    (kpool, vpool)[(n + w) // KH][
                        pl.ds((n + w) % KH * FB + c * per, per)
                    ].reshape(CF, TILE)
                    for w in range(wide)
                ]
                cols = slice(n * TILE, (n + wide) * TILE)
                acc[:, cols] += jnp.dot(
                    value, jnp.concatenate(right, axis=1), preferred_element_type=F32
                )

    for j in range(NJ + 1):
        if j < NJ:
            cols = slice(j * WC, (j + 1) * WC)
            down[:, cols] = acc[:, cols].astype(BF16)
            one_copy(j, *done_args).start()
        if j > 0:
            meet(j - 1, down, dn_one, dn_mid, done_args, dtwo_args)
    for j in range(NJ):
        cols = slice(j * WC, (j + 1) * WC)
        value = stream[:, cols] + acc[my_rows, cols] + dn_one[mid_own, cols].astype(F32)
        for k in range(1, NX):
            two_copy(k, j, *dtwo_args).wait_recv()
            value = value + dn_two[k - 1, :, cols].astype(F32)
        out[:, cols] = value.astype(BF16)
    result = pltpu.make_async_copy(out, out_hbm, in_sem.at[0])
    result.start()

    for j in range(NJ):
        one_copy(j, *one_args).wait_send()
        one_copy(j, *done_args).wait_send()
        for k in range(1, NX):
            two_copy(k, j, *two_args).wait_send()
            two_copy(k, j, *dtwo_args).wait_send()
            x_copy(k, j).wait_send()
        for k in range(NX):
            pair_copy(k, j).wait_send()

    for a in range(2):
        @pl.loop(0, nd)
        def _(origin):
            @pl.when(jnp.logical_and(me < E, origin <= me))
            def _():
                att_copy(origin, a, 0).wait_send()

            @pl.when(jnp.logical_and(me > 0, origin >= me))
            def _():
                att_copy(origin, a, 1).wait_send()

    for way in (0, 1):
        @pl.when(me != (E if way == 0 else 0))
        def _():
            ssd_copy(way).wait_send()

            @pl.loop(0, NC)
            def _(c):
                sum_copy(way, c).wait_send()
                hid_copy(way, c).wait_send()
    result.wait()


def solution(mesh):
    nd, nc = mesh.shape["dev"], mesh.shape["col"]

    def on_device(
        queries,
        kv_pages,
        page_table,
        seq_lengths,
        ffn_seat,
        resid,
        w_out,
        norm_gain,
        w_gate,
        w_up,
        w_down,
    ):
        B, HK = queries.shape
        blocks, kvl, _, page, head_dim = kv_pages.shape
        pages = page_table.shape[1]
        group = HK // (kvl * head_dim)
        heads = kvl * group
        T = ffn_seat.shape[0]
        R, DK = resid.shape
        FK = w_gate.shape[1]
        WC = divisor(DK, (512, 256, 128))
        NJ = DK // WC
        CF = divisor(FK, (256, 128))
        NC = FK // CF
        half = T // 2
        NX = nc // 2
        KB, FB = DK // TILE, FK // TILE
        dims = (
            T, B, R, HK, DK, FK, kvl, group, pages, blocks, WC, NJ, CF, NC, half, NX, float(DK * nd)
        )
        dma = pltpu.SemaphoreType.DMA
        hbm = pl.BlockSpec(memory_space=pltpu.HBM)
        vmem = pltpu.VMEM
        PB = B // 2
        scratch = [
            pltpu.SMEM((pages, B), jnp.int32),
            pltpu.SMEM((B,), jnp.int32),
            vmem((B, HK), BF16),
            vmem((1, T), jnp.int32),
            vmem((R, DK), BF16),
            vmem((1, DK), F32),
            vmem((HK, DK), BF16),
            vmem((DK, FK), BF16),
            vmem((DK, FK), BF16),
            vmem((max(blocks * kvl, (KB + 1) // 2 * FB), TILE, TILE), BF16),
            vmem((max(blocks * kvl, (KB + 1) // 2 * FB), TILE, TILE), BF16),
            vmem((B * heads, head_dim), F32),
            vmem((PB * heads, head_dim), F32),
            vmem((PB * heads, pages * page), F32),
            vmem((T, HK), BF16),
            vmem((T, HK), BF16),
            vmem((T, DK), BF16),
            vmem((NX * R, DK), BF16),
            vmem((NX * R, DK), BF16),
            vmem((max(NX - 1, 1), R, DK), BF16),
            vmem((T, DK), BF16),
            vmem((R, DK), F32),
            vmem((NC, 2, half, 2 * CF), BF16),
            vmem((NC, half, 2 * CF), BF16),
            vmem((NC, half, 2 * CF), BF16),
            vmem((T, 128), F32),
            vmem((half, 128), F32),
            vmem((half, 128), F32),
            vmem((half, 128), F32),
            vmem((NC, T, CF), BF16),
            vmem((T, DK), F32),
            vmem((T, DK), BF16),
            vmem((NX * R, DK), BF16),
            vmem((NX * R, DK), BF16),
            vmem((max(NX - 1, 1), R, DK), BF16),
            vmem((R, DK), BF16),
            dma((6,)),
            dma((2,)),
            dma((3 + KB,)),
            dma((2, nd, 2)),
            dma((nd, 2)),
            dma((NJ,)),
            dma((NJ,)),
            dma((max(NX - 1, 1), NJ)),
            dma((max(NX - 1, 1), NJ)),
            dma((max(NX - 1, 1), NJ)),
            dma((max(NX - 1, 1), NJ)),
            dma((NX, NJ)),
            dma((NX, NJ)),
            dma((2, NC)),
            dma((2, NC)),
            dma((2,)),
            dma((2,)),
            dma((2, NC)),
            dma((2, NC)),
            dma((NJ,)),
            dma((NJ,)),
            dma((max(NX - 1, 1), NJ)),
            dma((max(NX - 1, 1), NJ)),
        ]
        return pl.pallas_call(
            functools.partial(layer_kernel, nd, nc, dims),
            out_shape=jax.ShapeDtypeStruct((R, DK), BF16),
            in_specs=[hbm] * 11,
            out_specs=hbm,
            scratch_shapes=scratch,
            compiler_params=pltpu.CompilerParams(
                collective_id=0, has_side_effects=True, vmem_limit_bytes=67043328
            ),
        )(
            page_table.T,
            seq_lengths,
            queries,
            kv_pages.reshape(blocks * kvl, 2, page, head_dim),
            ffn_seat[None, :],
            resid,
            norm_gain[None, :],
            w_out,
            w_gate,
            w_up,
            w_down.reshape(FB, TILE, DK),
        )

    in_specs = (
        P(("rep", "dev"), "col"),
        P(("rep", "dev"), "col", None, None, None),
        P(("rep", "dev"), None),
        P(("rep", "dev")),
        P("rep"),
        P(("rep", "col"), "dev"),
        P("col", "dev"),
        P("dev"),
        P("dev", "col"),
        P("dev", "col"),
        P("col", "dev"),
    )
    return jax.shard_map(
        on_device,
        mesh=mesh,
        in_specs=in_specs,
        out_specs=P(("rep", "col"), "dev"),
        check_vma=False,
    )
```

time: 122 us -> 93.1 us (0.76)
  Pallas kernels: 116 us -> 91.3 us
  local copies, waits for them, and re-layouts: 6.11 us -> 1.57 us
    pallas_call x2 -> x1, Pallas kernels: 116 us -> 91.3 us  [on_device(): pl.pallas_call(functools.partial(layer_kernel, nd, nc, dims), out_shape=j...]
    unnamed x4 -> x1, local copies, waits for them, and re-layouts: 5.5 us -> 1.57 us
where the time goes in v1:
time: 93.1 us; the launch traced here: 92.9 us
  Pallas kernels  91.3 us (98%)
  local copies, waits for them, and re-layouts  1.57 us (2%)
    pallas_call x1, Pallas kernels, on_device(): pl.pallas_call(functools.partial(layer_kernel, nd, nc, dims), out_shape=j...  91.3 us

profile of v1, /device:TPU:0, one launch (start us, length us, event | category | flops | bytes accessed | tf_op | source)
XLA Modules:
  0.0 92.9 jit_solution(3402385571055617345)
XLA Ops:
  0.0 91.3 %shard_map.109 = bf16[32,2048]{1,0:T(8,128)(2,1)} custom-call(s32[3,32]{1,0:T(4,128)} %bitcast.8, s32[32]{0:T(128)} %len_hbm.1, bf16[32,2048]{1,0:T(8,128)(2,1)} %q_hbm.1, bf16[192,2,128,128]{3,2,1,0:T(8,128)(2,1)} %bitcast.6, s32[1,128]{1,0:T(1,128)} %bitcast.9, bf16[32,2048]{1,0:T(8,128)(2,1)} %resid_hbm.1, f32[1,2048]{1,0:T(1,128)} %bitcast.7, ...), custom_call_target="tpu_custom_call" | custom-call | tf_op jit(solution)/shard_map/pallas_call | solution.py:727
  91.3 1.6 %copy.13 = bf16[32,2048]{1,0:T(8,128)(2,1)} copy(bf16[32,2048]{1,0:T(8,128)(2,1)} %shard_map.109) | data formatting | bytes 262144

commit v2 on v1

--- a/solution.py
+++ b/solution.py
@@ -12,6 +12,7 @@
 BF16 = jnp.bfloat16
 TILE = 128
 SUB = 8
+LAG_S0, LAG_S, LAG_H0, LAG_H = 4, 3, 4, 5
 
 
 def divisor(size, choices):
@@ -176,7 +177,6 @@
     w_copies[0].start()
 
     neighbours = jnp.where(me > 0, 1, 0) + jnp.where(me < E, 1, 0)
-
     PB = B // 2
     scale = TILE ** (-0.5)
     head_row = lax.broadcasted_iota(jnp.int32, (heads, TILE), 0) // group
@@ -446,7 +446,7 @@
         ss_in = ss_r if way == 0 else ss_l
         ss_rows = pl.ds(part * half, half)
 
-        @pl.when(c == 0)
+        @pl.when(c == jnp.where(me == last, 0, min(1, NC - 1)))
         def _():
             ssd_copy(way).wait_recv()
             ss_own[ss_rows, :] = ss_own[ss_rows, :] + ss_in[...]
@@ -492,18 +492,18 @@
     PACE = 2
 
     def sum_lag(d):
-        return (5 * d + 1) // 2
-
-    first_hid = max(NC + 2, (5 * E + 1) // 2 + 1)
+        return LAG_S0 + LAG_S * (d - 1)
+
+    first_hid = max(NC + LAG_H0, sum_lag(E) + 1)
 
     def hid_lag(d):
-        return first_hid + (5 * (d - 1)) // 2
+        return first_hid + LAG_H * (d - 1)
 
     acc[...] = jnp.zeros_like(acc)
     w_copies[1].wait()
     w_copies[2].wait()
 
-    @pl.loop(0, NC + first_hid + (5 * (E - 1)) // 2)
+    @pl.loop(0, NC + hid_lag(E))
     def _(i):
         for p in range(PACE):
             q = i * PACE + p
@@ -622,6 +622,7 @@
             def _(c):
                 sum_copy(way, c).wait_send()
                 hid_copy(way, c).wait_send()
+
     result.wait()
 
 

time: 93.1 us -> 83.1 us (0.89)
  Pallas kernels: 91.3 us -> 81.4 us
    pallas_call x1, Pallas kernels: 91.3 us -> 81.4 us  [on_device(): pl.pallas_call(functools.partial(layer_kernel, nd, nc, dims), out_shape=j...]
where the time goes in v2:
time: 83.1 us; the launch traced here: 82.9 us
  Pallas kernels  81.4 us (98%)
  local copies, waits for them, and re-layouts  1.57 us (2%)
    pallas_call x1, Pallas kernels, on_device(): pl.pallas_call(functools.partial(layer_kernel, nd, nc, dims), out_shape=j...  81.4 us

profile of v2, /device:TPU:0, one launch (start us, length us, event | category | flops | bytes accessed | tf_op | source)
XLA Modules:
  0.0 82.9 jit_solution(4088821473981377906)
XLA Ops:
  0.0 81.4 %shard_map.109 = bf16[32,2048]{1,0:T(8,128)(2,1)} custom-call(s32[3,32]{1,0:T(4,128)} %bitcast.8, s32[32]{0:T(128)} %len_hbm.1, bf16[32,2048]{1,0:T(8,128)(2,1)} %q_hbm.1, bf16[192,2,128,128]{3,2,1,0:T(8,128)(2,1)} %bitcast.6, s32[1,128]{1,0:T(1,128)} %bitcast.9, bf16[32,2048]{1,0:T(8,128)(2,1)} %resid_hbm.1, f32[1,2048]{1,0:T(1,128)} %bitcast.7, ...), custom_call_target="tpu_custom_call" | custom-call | tf_op jit(solution)/shard_map/pallas_call | solution.py:728
  81.4 1.6 %copy.13 = bf16[32,2048]{1,0:T(8,128)(2,1)} copy(bf16[32,2048]{1,0:T(8,128)(2,1)} %shard_map.109) | data formatting | bytes 262144

commit v3 on v2

v3 whole, which is shorter than its diff:
```python
import functools

import jax
import jax.numpy as jnp
from jax import lax
from jax.experimental import pallas as pl
from jax.experimental.pallas import tpu as pltpu
from jax.sharding import PartitionSpec as P

MESH = pl.DeviceIdType.MESH
F32 = jnp.float32
BF16 = jnp.bfloat16
TILE = 128
SUB = 8
LATER = 3
PART = 2
WCM = 1024
LAG_S0 = 4
LAG_S = 3
LAG_H0 = 4
LAG_H = 5


def divisor(size, choices):
    for choice in choices:
        if size % choice == 0:
            return choice
    return size


def layer_kernel(
    nd,
    nc,
    dims,
    table_hbm,
    len_hbm,
    q_hbm,
    kv_hbm,
    seat_hbm,
    resid_hbm,
    gain_hbm,
    wo_hbm,
    wg_hbm,
    wu_hbm,
    wd_hbm,
    out,
    table,
    lens,
    q_in,
    seat,
    resid_all,
    resid_rows,
    pick,
    gain,
    wo,
    wg,
    wu,
    kpool,
    vpool,
    q_rows,
    o_rows,
    scores,
    att_all,
    proj,
    rs_one,
    rs_mid,
    rs_two,
    x_all,
    stream,
    own,
    in_r,
    in_l,
    ss_own,
    ss_r,
    ss_l,
    inv,
    hid,
    acc,
    down,
    dn_one,
    dn_mid,
    dn_two,
    in_sem,
    kv_sem,
    w_sem,
    att_s,
    att_r,
    res_s,
    res_r,
    one_s,
    one_r,
    two_s,
    two_r,
    x_s,
    x_r,
    pair_s,
    pair_r,
    sum_s,
    sum_r,
    ssd_s,
    ssd_r,
    hid_s,
    hid_r,
    done_s,
    done_r,
    dtwo_s,
    dtwo_r,
):
    T, B, R, HK, DK, FK, kvl, group, pages, blocks, WC, NJ, CF, NC, half, NX, full = dims
    RH = half // nc
    PACE = 2
    PHASE = (NC + PACE - 1) // PACE
    me = lax.axis_index("dev")
    mc = lax.axis_index("col")
    mx, core = mc // 2, mc % 2
    E = nd - 1
    late_dev = (me * 2) // nd
    halves = (late_dev, 1 - late_dev)
    heads = kvl * group
    span = pages * TILE
    KB = DK // TILE
    FB = FK // TILE
    KH = (KB + 1) // 2
    partner = {"col": mx * 2 + 1 - core}

    def peer_of(k):
        return lax.rem(mc + k, nc)

    def x_peer(k):
        return lax.rem(mx + k, NX)

    def x_from(k):
        return lax.rem(mx + NX - k, NX)

    small = [
        pltpu.make_async_copy(table_hbm, table, in_sem.at[0]),
        pltpu.make_async_copy(len_hbm, lens, in_sem.at[1]),
        pltpu.make_async_copy(q_hbm, q_in, in_sem.at[2]),
        pltpu.make_async_copy(seat_hbm, seat, in_sem.at[3]),
        pltpu.make_async_copy(
            resid_hbm, resid_all.at[pl.ds(pl.multiple_of(mc * R, R), R), :], in_sem.at[4]
        ),
        pltpu.make_async_copy(gain_hbm, gain, in_sem.at[5]),
    ]
    kv_count = blocks * kvl
    kv_copies = [
        pltpu.make_async_copy(
            kv_hbm.at[:, v], (kpool, vpool)[v].at[pl.ds(0, kv_count)], kv_sem.at[v]
        )
        for v in (0, 1)
    ]
    w_copies = [
        pltpu.make_async_copy(wo_hbm, wo, w_sem.at[0]),
        pltpu.make_async_copy(wg_hbm, wg, w_sem.at[1]),
        pltpu.make_async_copy(wu_hbm, wu, w_sem.at[2]),
    ]

    def wd_copy(n):
        cols = slice(n * TILE, (n + 1) * TILE)
        return pltpu.make_async_copy(
            wd_hbm.at[:, :, cols],
            (kpool, vpool)[n // KH].at[pl.ds(n % KH * FB, FB)],
            w_sem.at[3 + n // KH],
        )

    def wd_wait():
        for n, target in enumerate((kpool, vpool)):
            count = min(KH, KB - n * KH)
            if count > 0:
                spot = target.at[pl.ds(0, count * FB)]
                pltpu.make_async_copy(spot, spot, w_sem.at[3 + n]).wait()

    for copy in small:
        copy.start()
    for copy in kv_copies:
        copy.start()

    barrier = pltpu.get_barrier_semaphore()

    @pl.when(me > 0)
    def _():
        pl.semaphore_signal(barrier, inc=1, device_id={"dev": me - 1}, device_id_type=MESH)

    @pl.when(me < E)
    def _():
        pl.semaphore_signal(barrier, inc=1, device_id={"dev": me + 1}, device_id_type=MESH)

    for k in range(1, nc):
        pl.semaphore_signal(barrier, inc=1, device_id={"col": peer_of(k)}, device_id_type=MESH)

    small[2].wait()
    for n in range(heads):
        q_rows[pl.ds(n, B, stride=heads), :] = q_in[:, n * TILE : (n + 1) * TILE].astype(F32)
    small[0].wait()
    small[1].wait()
    def res_copy(k):
        spot = resid_all.at[pl.ds(pl.multiple_of(mc * R, R), R), :]
        return pltpu.make_async_remote_copy(
            src_ref=spot,
            dst_ref=spot,
            send_sem=res_s.at[k - 1],
            recv_sem=res_r.at[k - 1],
            device_id={"col": peer_of(k)},
            device_id_type=MESH,
        )

    neighbours = jnp.where(me > 0, 1, 0) + jnp.where(me < E, 1, 0)
    for copy in small[3:]:
        copy.wait()
    pl.semaphore_wait(barrier, neighbours + nc - 1)
    for k in range(1, nc):
        res_copy(k).start()
    kv_copies[0].wait()
    w_copies[0].start()

    PB = B // 2
    scale = TILE ** (-0.5)
    head_row = lax.broadcasted_iota(jnp.int32, (heads, TILE), 0) // group

    def blocked(value):
        if kvl == 1:
            return value.astype(BF16)
        wide = lax.broadcasted_iota(jnp.int32, value.shape, 0) // group
        return jnp.concatenate(
            [jnp.where(wide == h, value, 0.0).astype(BF16) for h in range(kvl)], axis=1
        )

    def att_copy(origin, a, way):
        spot = att_all.at[pl.ds(pl.multiple_of(origin * B + a * PB, PB), PB), :]
        return pltpu.make_async_remote_copy(
            src_ref=spot,
            dst_ref=spot,
            send_sem=att_s.at[way, origin, a],
            recv_sem=att_r.at[origin, a],
            device_id={"dev": me + (1 if way == 0 else -1)},
            device_id_type=MESH,
        )

    if True:
        @pl.loop(0, B // SUB)
        def _(b):
            for u in range(SUB):
                s = spot = b * SUB + u
                rows = pl.ds(pl.multiple_of(s * heads, heads), heads)
                query = blocked(q_rows[rows, :])
                keys = []
                for j in range(pages):
                    block = table[j, s]
                    keys.append(
                        jnp.concatenate([kpool[block * kvl + h] for h in range(kvl)], axis=1)
                        if kvl > 1
                        else kpool[block]
                    )
                value = lax.dot_general(
                    query,
                    jnp.concatenate(keys, axis=0),
                    (((1,), (1,)), ((), ())),
                    preferred_element_type=F32,
                ) * scale
                live = lax.broadcasted_iota(jnp.int32, value.shape, 1) < lens[s]
                scores[pl.ds(pl.multiple_of(spot * heads, heads), heads), :] = jnp.where(
                    live, value, -1e30
                )

    kv_copies[1].wait()
    w_copies[1].start()
    w_copies[2].start()
    for a in range(2):

        @pl.loop(0, PB // SUB)
        def _(b):
            base = a * PB + b * SUB
            rows = pl.ds(pl.multiple_of(base * heads, SUB * heads), SUB * heads)
            value = scores[rows, :]
            expo = jnp.exp(value - jnp.max(value, axis=1, keepdims=True))
            scores[rows, :] = expo / jnp.sum(expo, axis=1, keepdims=True)
            for u in range(SUB):
                spot = b * SUB + u
                s = a * PB + spot
                weights = blocked(scores[pl.ds(pl.multiple_of(s * heads, heads), heads), :])
                vals = [
                    vpool[table[j, s] * kvl + h]
                    for h in range(kvl)
                    for j in range(pages)
                ]
                o_rows[pl.ds(pl.multiple_of(spot * heads, heads), heads), :] = jnp.dot(
                    weights, jnp.concatenate(vals, axis=0), preferred_element_type=F32
                )

        mine = pl.ds(pl.multiple_of(me * B + a * PB, PB), PB)
        for n in range(heads):
            att_all[mine, n * TILE : (n + 1) * TILE] = o_rows[
                pl.ds(n, PB, stride=heads), :
            ].astype(BF16)

        @pl.when(me < E)
        def _():
            att_copy(me, a, 0).start()

        @pl.when(me > 0)
        def _():
            att_copy(me, a, 1).start()

    for n in range(KB):
        wd_copy(n).start()

    place = lax.broadcasted_iota(jnp.int32, (T, T), 0)
    position = place // R
    seat_here = ((position % NX) * 2 + position // NX) * R + place % R
    pick[...] = (seat_here == seat[...]).astype(F32).astype(BF16)
    fetch = (place == seat[...]).astype(F32).astype(BF16)

    def from_left(k, pass_on):
        for a in range(2):
            att_copy(me - k, a, 0).wait_recv()
            if pass_on:
                att_copy(me - k, a, 0).start()

    def from_right(k, pass_on):
        for a in range(2):
            att_copy(me + k, a, 1).wait_recv()
            if pass_on:
                att_copy(me + k, a, 1).start()

    def ends(k):
        @pl.when(jnp.logical_and(me == E, me - k >= 0))
        def _():
            from_left(k, False)

        @pl.when(jnp.logical_and(me == 0, me + k <= E))
        def _():
            from_right(k, False)

    def relay(k):
        @pl.when(jnp.logical_and(me < E, me - k >= 0))
        def _():
            from_left(k, True)

        @pl.when(jnp.logical_and(me > 0, me + k <= E))
        def _():
            from_right(k, True)

    @pl.loop(1, nd // 2)
    def _(k):
        relay(k)
        ends(k)

    half_rows = NX * RH

    def rows_of(step, c, x, count=1):
        start = halves[step] * half + (c * NX + x) * RH
        return pl.ds(pl.multiple_of(start, RH), count * RH)

    mid_own = pl.ds(pl.multiple_of(mx * RH, RH), RH)

    def whole(spot, send, recv):
        return pltpu.make_async_remote_copy(
            src_ref=spot,
            dst_ref=spot,
            send_sem=send,
            recv_sem=recv,
            device_id=partner,
            device_id_type=MESH,
        )

    def one_copy(step, j):
        cols = slice(j * WC, (j + 1) * WC)
        return pltpu.make_async_remote_copy(
            src_ref=proj.at[rows_of(step, 1 - core, 0, NX), cols],
            dst_ref=rs_one.at[step, :, cols],
            send_sem=one_s.at[step],
            recv_sem=one_r.at[step, j],
            device_id=partner,
            device_id_type=MESH,
        )

    def two_copy(step, k, j):
        cols = slice(j * WC, (j + 1) * WC)
        rows = pl.ds(pl.multiple_of(x_peer(k) * RH, RH), RH)
        return pltpu.make_async_remote_copy(
            src_ref=rs_mid.at[step, rows, cols],
            dst_ref=rs_two.at[step, k - 1, :, cols],
            send_sem=two_s.at[step, k - 1],
            recv_sem=two_r.at[step, k - 1, j],
            device_id={"col": x_peer(k) * 2 + core},
            device_id_type=MESH,
        )

    def project(step, j):
        cols = slice(j * WC, (j + 1) * WC)
        rows = pl.ds(pl.multiple_of(halves[step] * half, half), half)
        proj[rows, cols] = jnp.dot(
            att_all[rows, :], wo[:, cols], preferred_element_type=F32
        ).astype(BF16)
        one_copy(step, j).start()

    def meet(step, j):
        cols = slice(j * WC, (j + 1) * WC)
        one_copy(step, j).wait_recv()
        rs_mid[step, :, cols] = (
            proj[rows_of(step, core, 0, NX), cols].astype(F32) + rs_one[step, :, cols].astype(F32)
        ).astype(BF16)
        for k in range(1, NX):
            two_copy(step, k, j).start()

    def x_copy(step, k, j):
        spot = x_all.at[rows_of(step, core, mx), j * WC : (j + 1) * WC]
        return pltpu.make_async_remote_copy(
            src_ref=spot,
            dst_ref=spot,
            send_sem=x_s.at[step, k - 1],
            recv_sem=x_r.at[step, k - 1, j],
            device_id={"col": x_peer(k) * 2 + core},
            device_id_type=MESH,
        )

    def pair_copy(step, k, j):
        spot = x_all.at[rows_of(step, core, x_from(k)), j * WC : (j + 1) * WC]
        return pltpu.make_async_remote_copy(
            src_ref=spot,
            dst_ref=spot,
            send_sem=pair_s.at[step, k],
            recv_sem=pair_r.at[step],
            device_id=partner,
            device_id_type=MESH,
        )

    def streams(step):
        own_rows = rows_of(step, core, mx)
        for j in range(NJ):
            cols = slice(j * WC, (j + 1) * WC)
            value = (
                resid_rows[own_rows, cols].astype(F32)
                + proj[own_rows, cols].astype(F32)
                + rs_one[step, mid_own, cols].astype(F32)
            )
            for k in range(1, NX):
                two_copy(step, k, j).wait_recv()
                value = value + rs_two[step, k - 1, :, cols].astype(F32)
            stream[step, :, cols] = value
            x_all[own_rows, cols] = (value * gain[:, cols]).astype(BF16)
            for k in range(1, NX):
                x_copy(step, k, j).start()
            pair_copy(step, 0, j).start()

    def x_forward(step):
        for j in range(NJ):
            for k in range(1, NX):
                x_copy(step, k, j).wait_recv()
                pair_copy(step, k, j).start()

    def x_arrive(step):
        spot = x_all.at[rows_of(step, 1 - core, 0, NX), :]
        whole(spot, pair_s.at[step, 0], pair_r.at[step]).wait_recv()

    w_copies[0].wait()
    for j in range(NJ + 1):
        if j < NJ:
            project(0, j)
        if j > 0:
            meet(0, j - 1)

    @pl.loop(nd // 2, nd)
    def _(k):
        relay(k)

    for k in range(1, nc):
        res_copy(k).wait_recv()
    for j in range(NJ):
        cols = slice(j * WC, (j + 1) * WC)
        resid_rows[:, cols] = lax.dot_general(
            fetch, resid_all[:, cols], (((0,), (0,)), ((), ())), preferred_element_type=F32
        ).astype(BF16)
    streams(0)

    @pl.loop(nd // 2, nd)
    def _(k):
        ends(k)

    for j in range(NJ):
        project(1, j)
    x_forward(0)
    for j in range(NJ):
        meet(1, j)
    x_arrive(0)
    def neighbour(way):
        return {"dev": me + (1 if way == 0 else -1)}

    RQ = half // PART

    def sum_copy(way, c, r):
        rows = slice(r * RQ, (r + 1) * RQ)
        return pltpu.make_async_remote_copy(
            src_ref=own.at[c, way, rows, :],
            dst_ref=(in_r if way == 0 else in_l).at[c, rows, :],
            send_sem=sum_s.at[way],
            recv_sem=sum_r.at[way, c, r],
            device_id=neighbour(way),
            device_id_type=MESH,
        )

    def ssd_copy(way):
        return pltpu.make_async_remote_copy(
            src_ref=ss_own.at[pl.ds(way * half, half), :],
            dst_ref=ss_r if way == 0 else ss_l,
            send_sem=ssd_s.at[way],
            recv_sem=ssd_r.at[way],
            device_id=neighbour(way),
            device_id_type=MESH,
        )

    def hid_copy(way, c, r):
        spot = hid.at[c, pl.ds((1 - way) * half + r * RQ, RQ), :]
        return pltpu.make_async_remote_copy(
            src_ref=spot,
            dst_ref=spot,
            send_sem=hid_s.at[way],
            recv_sem=hid_r.at[way, c, r],
            device_id=neighbour(way),
            device_id_type=MESH,
        )

    def sum_stage(way, c):
        first = 0 if way == 0 else E
        last = E - first
        part = way
        incoming = in_r if way == 0 else in_l
        ss_in = ss_r if way == 0 else ss_l
        ss_rows = pl.ds(part * half, half)

        @pl.when(c == jnp.where(me == last, 0, min(1, NC - 1)))
        def _():
            ssd_copy(way).wait_recv()
            ss_own[ss_rows, :] = ss_own[ss_rows, :] + ss_in[...]

            @pl.when(me != last)
            def _():
                ssd_copy(way).start()

            @pl.when(me == last)
            def _():
                inv[...] = lax.rsqrt(ss_own[ss_rows, :] / full + 1e-5)

        for r in range(PART):
            rows = slice(r * RQ, (r + 1) * RQ)
            sum_copy(way, c, r).wait_recv()
            total = own[c, part, rows, :].astype(F32) + incoming[c, rows, :].astype(F32)

            @pl.when(me != last)
            def _():
                own[c, part, rows, :] = total.astype(BF16)
                sum_copy(way, c, r).start()

            @pl.when(me == last)
            def _():
                factor = inv[rows, 0:1]
                gate = total[:, :CF] * factor
                up = total[:, CF:] * factor
                hid[c, part * half + r * RQ : part * half + (r + 1) * RQ, :] = (
                    gate / (1.0 + jnp.exp(-gate)) * up
                ).astype(BF16)
                hid_copy(1 - way, c, r).start()

    def hid_stage(way, c):
        last = E if way == 0 else 0
        for r in range(PART):
            hid_copy(way, c, r).wait_recv()

            @pl.when(me != last)
            def _():
                hid_copy(way, c, r).start()

    def inside(c):
        return jnp.logical_and(c >= 0, c < NC)

    def sum_lag(d):
        return LAG_S0 + LAG_S * (d - 1)

    first_hid = max(NC + LAG_H0, sum_lag(E) + 1)

    def hid_lag(d):
        return first_hid + LAG_H * (d - 1)

    acc[...] = jnp.zeros_like(acc)
    w_copies[1].wait()
    w_copies[2].wait()

    @pl.loop(0, NC + hid_lag(E))
    def _(i):
        group = i // PHASE
        turn = halves[0] + group * (halves[1] - halves[0])
        turn_rows = pl.ds(pl.multiple_of(turn * half, half), half)

        @pl.when(i == min(LATER, PHASE))
        def _():
            streams(1)

        @pl.when(i == min(LATER + 3, PHASE))
        def _():
            x_forward(1)

        @pl.when(i == PHASE)
        def _():
            x_arrive(1)
        for p in range(PACE):
            q = (i - group * PHASE) * PACE + p

            @pl.when(jnp.logical_and(group < 2, q < NC))
            def _():
                cols = pl.ds(pl.multiple_of(q * CF, CF), CF)
                value = x_all[turn_rows, :]
                own[q, turn, :, :CF] = jnp.dot(
                    value, wg[:, cols], preferred_element_type=F32
                ).astype(BF16)
                own[q, turn, :, CF:] = jnp.dot(
                    value, wu[:, cols], preferred_element_type=F32
                ).astype(BF16)
                for way in (0, 1):
                    @pl.when(jnp.logical_and(group == 0, me == (0 if way == 0 else E)))
                    def _():
                        for r in range(PART):
                            sum_copy(way, q, r).start()

        @pl.when(jnp.logical_and(group < 2, i == group * PHASE))
        def _():
            squares = jnp.zeros((half, 1), F32)
            for j in range(NJ):
                cols = slice(j * WC, (j + 1) * WC)
                value = x_all[turn_rows, cols].astype(F32) / gain[:, cols]
                squares = squares + jnp.sum(value * value, axis=1, keepdims=True)
            ss_own[turn_rows, :] = jnp.broadcast_to(squares, (half, ss_own.shape[1]))
            for way in (0, 1):
                @pl.when(jnp.logical_and(group == 0, me == (0 if way == 0 else E)))
                def _():
                    ssd_copy(way).start()

        for way in (0, 1):
            d = me if way == 0 else E - me
            c = i - sum_lag(d)

            @pl.when(jnp.logical_and(d > 0, inside(c)))
            def _():
                sum_stage(way, c)

        for way in (0, 1):
            d = me if way == 0 else E - me
            c = i - hid_lag(d)

            @pl.when(jnp.logical_and(d > 0, inside(c)))
            def _():
                hid_stage(way, c)

        c = i - hid_lag(jnp.maximum(me, E - me))

        @pl.when(i == hid_lag(jnp.maximum(me, E - me)))
        def _():
            wd_wait()

        @pl.when(inside(c))
        def _():
            per = CF // TILE
            wide = 2 if KB % 2 == 0 else 1
            value = hid[c]
            for n in range(0, KB, wide):
                right = [
                    (kpool, vpool)[(n + w) // KH][
                        pl.ds((n + w) % KH * FB + c * per, per)
                    ].reshape(CF, TILE)
                    for w in range(wide)
                ]
                cols = slice(n * TILE, (n + wide) * TILE)
                acc[:, cols] += jnp.dot(
                    value, jnp.concatenate(right, axis=1), preferred_element_type=F32
                )

    my_half = pl.ds(pl.multiple_of(core * NX * R, R), NX * R)
    other_half = pl.ds(pl.multiple_of((1 - core) * NX * R, R), NX * R)

    def done_copy(j):
        cols = slice(j * WC, (j + 1) * WC)
        return pltpu.make_async_remote_copy(
            src_ref=down.at[other_half, cols],
            dst_ref=dn_one.at[:, cols],
            send_sem=done_s.at[0],
            recv_sem=done_r.at[j],
            device_id=partner,
            device_id_type=MESH,
        )

    def last_copy(k, j):
        cols = slice(j * WC, (j + 1) * WC)
        rows = pl.ds(pl.multiple_of(x_peer(k) * R, R), R)
        return pltpu.make_async_remote_copy(
            src_ref=dn_mid.at[rows, cols],
            dst_ref=dn_two.at[k - 1, :, cols],
            send_sem=dtwo_s.at[k - 1],
            recv_sem=dtwo_r.at[k - 1, j],
            device_id={"col": x_peer(k) * 2 + core},
            device_id_type=MESH,
        )

    for step in (0, 1):
        rows = rows_of(step, core, mx)
        acc[rows, :] = acc[rows, :] + stream[step]
    for j in range(NJ + 1):
        if j < NJ:
            cols = slice(j * WC, (j + 1) * WC)
            down[:, cols] = jnp.dot(
                pick[...], acc[:, cols].astype(BF16), preferred_element_type=F32
            ).astype(BF16)
            done_copy(j).start()
        if j > 0:
            cols = slice((j - 1) * WC, j * WC)
            done_copy(j - 1).wait_recv()
            dn_mid[:, cols] = (
                down[my_half, cols].astype(F32) + dn_one[:, cols].astype(F32)
            ).astype(BF16)
            for k in range(1, NX):
                last_copy(k, j - 1).start()
    my_rows = pl.ds(pl.multiple_of((core * NX + mx) * R, R), R)
    my_mid = pl.ds(pl.multiple_of(mx * R, R), R)
    for j in range(NJ):
        cols = slice(j * WC, (j + 1) * WC)
        value = down[my_rows, cols].astype(F32) + dn_one[my_mid, cols].astype(F32)
        for k in range(1, NX):
            last_copy(k, j).wait_recv()
            value = value + dn_two[k - 1, :, cols].astype(F32)
        out[:, cols] = value.astype(BF16)

    for k in range(1, nc):
        res_copy(k).wait_send()
    for step in (0, 1):
        mine = x_all.at[rows_of(step, core, mx), :]
        whole(proj.at[rows_of(step, 1 - core, 0, NX), :], one_s.at[step], one_r.at[step, 0]).wait_send()
        for k in range(1, NX):
            whole(mine, two_s.at[step, k - 1], one_r.at[step, 0]).wait_send()
            whole(mine, x_s.at[step, k - 1], one_r.at[step, 0]).wait_send()
        for k in range(NX):
            whole(mine, pair_s.at[step, k], one_r.at[step, 0]).wait_send()
    whole(down.at[other_half, :], done_s.at[0], done_r.at[0]).wait_send()
    for k in range(1, NX):
        whole(down.at[my_rows, :], dtwo_s.at[k - 1], done_r.at[0]).wait_send()

    for a in range(2):
        @pl.loop(0, nd)
        def _(origin):
            @pl.when(jnp.logical_and(me < E, origin <= me))
            def _():
                att_copy(origin, a, 0).wait_send()

            @pl.when(jnp.logical_and(me > 0, origin >= me))
            def _():
                att_copy(origin, a, 1).wait_send()

    for way in (0, 1):
        @pl.when(me != (E if way == 0 else 0))
        def _():
            ssd_copy(way).wait_send()

            whole(own.at[:, way], sum_s.at[way], sum_r.at[way, 0, 0]).wait_send()
            sent = hid.at[:, pl.ds((1 - way) * half, half), :]
            whole(sent, hid_s.at[way], hid_r.at[way, 0, 0]).wait_send()


def solution(mesh):
    nd, nc = mesh.shape["dev"], mesh.shape["col"]

    def on_device(
        queries,
        kv_pages,
        page_table,
        seq_lengths,
        ffn_seat,
        resid,
        w_out,
        norm_gain,
        w_gate,
        w_up,
        w_down,
    ):
        B, HK = queries.shape
        blocks, kvl, _, page, head_dim = kv_pages.shape
        pages = page_table.shape[1]
        group = HK // (kvl * head_dim)
        heads = kvl * group
        T = ffn_seat.shape[0]
        R, DK = resid.shape
        FK = w_gate.shape[1]
        WC = divisor(DK, (WCM, 512, 256, 128))
        NJ = DK // WC
        CF = divisor(FK, (256, 128))
        NC = FK // CF
        half = T // 2
        NX = nc // 2
        KB, FB = DK // TILE, FK // TILE
        dims = (
            T, B, R, HK, DK, FK, kvl, group, pages, blocks, WC, NJ, CF, NC, half, NX, float(DK * nd)
        )
        dma = pltpu.SemaphoreType.DMA
        hbm = pl.BlockSpec(memory_space=pltpu.HBM)
        vmem = pltpu.VMEM
        PB = B // 2
        scratch = [
            pltpu.SMEM((pages, B), jnp.int32),
            pltpu.SMEM((B,), jnp.int32),
            vmem((B, HK), BF16),
            vmem((1, T), jnp.int32),
            vmem((T, DK), BF16),
            vmem((T, DK), BF16),
            vmem((T, T), BF16),
            vmem((1, DK), F32),
            vmem((HK, DK), BF16),
            vmem((DK, FK), BF16),
            vmem((DK, FK), BF16),
            vmem((max(blocks * kvl, (KB + 1) // 2 * FB), TILE, TILE), BF16),
            vmem((max(blocks * kvl, (KB + 1) // 2 * FB), TILE, TILE), BF16),
            vmem((B * heads, head_dim), F32),
            vmem((PB * heads, head_dim), F32),
            vmem((B * heads, pages * page), F32),
            vmem((T, HK), BF16),
            vmem((T, DK), BF16),
            vmem((2, half // 2, DK), BF16),
            vmem((2, half // 2, DK), BF16),
            vmem((2, max(NX - 1, 1), half // nc, DK), BF16),
            vmem((T, DK), BF16),
            vmem((2, half // nc, DK), F32),
            vmem((NC, 2, half, 2 * CF), BF16),
            vmem((NC, half, 2 * CF), BF16),
            vmem((NC, half, 2 * CF), BF16),
            vmem((T, 128), F32),
            vmem((half, 128), F32),
            vmem((half, 128), F32),
            vmem((half, 128), F32),
            vmem((NC, T, CF), BF16),
            vmem((T, DK), F32),
            vmem((T, DK), BF16),
            vmem((NX * R, DK), BF16),
            vmem((NX * R, DK), BF16),
            vmem((max(NX - 1, 1), R, DK), BF16),
            dma((6,)),
            dma((2,)),
            dma((5,)),
            dma((2, nd, 2)),
            dma((nd, 2)),
            dma((nc - 1,)),
            dma((nc - 1,)),
            dma((2,)),
            dma((2, NJ)),
            dma((2, max(NX - 1, 1))),
            dma((2, max(NX - 1, 1), NJ)),
            dma((2, max(NX - 1, 1))),
            dma((2, max(NX - 1, 1), NJ)),
            dma((2, NX)),
            dma((2,)),
            dma((2,)),
            dma((2, NC, PART)),
            dma((2,)),
            dma((2,)),
            dma((2,)),
            dma((2, NC, PART)),
            dma((1,)),
            dma((NJ,)),
            dma((max(NX - 1, 1),)),
            dma((max(NX - 1, 1), NJ)),
        ]
        return pl.pallas_call(
            functools.partial(layer_kernel, nd, nc, dims),
            out_shape=pltpu.VMEM((R, DK), BF16),
            in_specs=[hbm] * 11,
            out_specs=pl.BlockSpec(memory_space=pltpu.VMEM),
            scratch_shapes=scratch,
            compiler_params=pltpu.CompilerParams(
                collective_id=0, has_side_effects=True, vmem_limit_bytes=65 * 1000 * 1000
            ),
        )(
            page_table.T,
            seq_lengths,
            queries,
            kv_pages.reshape(blocks * kvl, 2, page, head_dim),
            ffn_seat[None, :],
            resid,
            norm_gain[None, :],
            w_out,
            w_gate,
            w_up,
            w_down.reshape(FB, TILE, DK),
        )

    in_specs = (
        P(("rep", "dev"), "col"),
        P(("rep", "dev"), "col", None, None, None),
        P(("rep", "dev"), None),
        P(("rep", "dev")),
        P("rep"),
        P(("rep", "col"), "dev"),
        P("col", "dev"),
        P("dev"),
        P("dev", "col"),
        P("dev", "col"),
        P("col", "dev"),
    )
    return jax.shard_map(
        on_device,
        mesh=mesh,
        in_specs=in_specs,
        out_specs=P(("rep", "col"), "dev"),
        check_vma=False,
    )
```

time: 83.1 us -> 74.1 us (0.89)
  Pallas kernels: 81.4 us -> 73.3 us
  local copies, waits for them, and re-layouts: 1.57 us -> 0.66 us
    pallas_call x1, Pallas kernels: 81.4 us -> 73.3 us  [on_device(): pl.pallas_call(functools.partial(layer_kernel, nd, nc, dims), out_shape=p...]
    unnamed x1, local copies, waits for them, and re-layouts: 1.57 us -> 0.66 us
where the time goes in v3:
time: 74.1 us; the launch traced here: 74 us
  Pallas kernels  73.3 us (99%)
    pallas_call x1, Pallas kernels, on_device(): pl.pallas_call(functools.partial(layer_kernel, nd, nc, dims), out_shape=p...  73.3 us

profile of v3, /device:TPU:0, one launch (start us, length us, event | category | flops | bytes accessed | tf_op | source)
XLA Modules:
  0.0 74.0 jit_solution(17277221287372805095)
XLA Ops:
  0.0 73.3 %shard_map.109 = bf16[32,2048]{1,0:T(8,128)(2,1)S(1)} custom-call(s32[3,32]{1,0:T(4,128)} %bitcast.8, s32[32]{0:T(128)} %len_hbm.1, bf16[32,2048]{1,0:T(8,128)(2,1)} %q_hbm.1, bf16[192,2,128,128]{3,2,1,0:T(8,128)(2,1)} %bitcast.6, s32[1,128]{1,0:T(1,128)} %bitcast.9, bf16[32,2048]{1,0:T(8,128)(2,1)} %resid_hbm.1, f32[1,2048]{1,0:T(1,128)} %bitcast.7, ...), custom_call_target="tpu_custom_call" | custom-call | tf_op jit(solution)/shard_map/pallas_call | solution.py:866
  73.3 0.7 copy.13

commit v4 on v3

--- a/solution.py
+++ b/solution.py
@@ -12,8 +12,10 @@
 BF16 = jnp.bfloat16
 TILE = 128
 SUB = 8
-LATER = 3
-PART = 2
+LATER = 5
+END_PROJ = 2
+END_GAP = 2
+PART = 1
 WCM = 1024
 LAG_S0 = 4
 LAG_S = 3
@@ -76,7 +78,6 @@
     inv,
     hid,
     acc,
-    down,
     dn_one,
     dn_mid,
     dn_two,
@@ -85,14 +86,13 @@
     w_sem,
     att_s,
     att_r,
+    far_s,
     res_s,
     res_r,
     one_s,
     one_r,
     two_s,
     two_r,
-    x_s,
-    x_r,
     pair_s,
     pair_r,
     sum_s,
@@ -108,8 +108,10 @@
 ):
     T, B, R, HK, DK, FK, kvl, group, pages, blocks, WC, NJ, CF, NC, half, NX, full = dims
     RH = half // nc
-    PACE = 2
-    PHASE = (NC + PACE - 1) // PACE
+    PACE = 2 if NC % 2 == 0 else 1
+    PHASE = NC // PACE
+    MID_START = max(PHASE, LATER + 2)
+    END_START = MID_START + END_GAP
     me = lax.axis_index("dev")
     mc = lax.axis_index("col")
     mx, core = mc // 2, mc % 2
@@ -185,6 +187,11 @@
     def _():
         pl.semaphore_signal(barrier, inc=1, device_id={"dev": me + 1}, device_id_type=MESH)
 
+    for here, there in ((E - 2, E), (E, E - 2), (2, 0), (0, 2)):
+        @pl.when(me == here)
+        def _():
+            pl.semaphore_signal(barrier, inc=1, device_id={"dev": there}, device_id_type=MESH)
+
     for k in range(1, nc):
         pl.semaphore_signal(barrier, inc=1, device_id={"col": peer_of(k)}, device_id_type=MESH)
 
@@ -205,6 +212,8 @@
         )
 
     neighbours = jnp.where(me > 0, 1, 0) + jnp.where(me < E, 1, 0)
+    for here in (E - 2, E, 2, 0):
+        neighbours = neighbours + jnp.where(me == here, 1, 0)
     for copy in small[3:]:
         copy.wait()
     pl.semaphore_wait(barrier, neighbours + nc - 1)
@@ -265,6 +274,18 @@
     kv_copies[1].wait()
     w_copies[1].start()
     w_copies[2].start()
+    def far_copy(way, a):
+        origin = 0 if way == 0 else E
+        spot = att_all.at[pl.ds(origin * B + a * PB, PB), :]
+        return pltpu.make_async_remote_copy(
+            src_ref=spot,
+            dst_ref=spot,
+            send_sem=far_s.at[way, a],
+            recv_sem=att_r.at[origin, a],
+            device_id={"dev": E - origin},
+            device_id_type=MESH,
+        )
+
     for a in range(2):
 
         @pl.loop(0, PB // SUB)
@@ -310,40 +331,39 @@
     pick[...] = (seat_here == seat[...]).astype(F32).astype(BF16)
     fetch = (place == seat[...]).astype(F32).astype(BF16)
 
-    def from_left(k, pass_on):
-        for a in range(2):
-            att_copy(me - k, a, 0).wait_recv()
-            if pass_on:
-                att_copy(me - k, a, 0).start()
-
-    def from_right(k, pass_on):
-        for a in range(2):
-            att_copy(me + k, a, 1).wait_recv()
-            if pass_on:
-                att_copy(me + k, a, 1).start()
-
-    def ends(k):
-        @pl.when(jnp.logical_and(me == E, me - k >= 0))
-        def _():
-            from_left(k, False)
-
-        @pl.when(jnp.logical_and(me == 0, me + k <= E))
-        def _():
-            from_right(k, False)
-
-    def relay(k):
-        @pl.when(jnp.logical_and(me < E, me - k >= 0))
-        def _():
-            from_left(k, True)
-
-        @pl.when(jnp.logical_and(me > 0, me + k <= E))
-        def _():
-            from_right(k, True)
+    def passes(origin, way):
+        if way == 0:
+            return jnp.logical_and(me < E, jnp.logical_or(origin > 0, me + 1 < E))
+        return jnp.logical_and(me > 0, jnp.logical_or(origin < E, me - 1 > 0))
+
+    def take(origin, way, relay):
+        inside = origin >= 0 if way == 0 else origin <= E
+        move = passes(origin, way)
+        wanted = move if relay else jnp.logical_not(move)
+
+        @pl.when(jnp.logical_and(inside, wanted))
+        def _():
+            for a in range(2):
+                att_copy(origin, a, way).wait_recv()
+                if relay:
+                    att_copy(origin, a, way).start()
+
+                    @pl.when(
+                        jnp.logical_and(
+                            me == (E - 2 if way == 0 else 2), origin == (0 if way == 0 else E)
+                        )
+                    )
+                    def _():
+                        far_copy(way, a).start()
+
+    def both(k, relay):
+        take(me - k, 0, relay)
+        take(me + k, 1, relay)
 
     @pl.loop(1, nd // 2)
     def _(k):
-        relay(k)
-        ends(k)
+        both(k, True)
+        both(k, False)
 
     half_rows = NX * RH
 
@@ -376,9 +396,8 @@
 
     def two_copy(step, k, j):
         cols = slice(j * WC, (j + 1) * WC)
-        rows = pl.ds(pl.multiple_of(x_peer(k) * RH, RH), RH)
-        return pltpu.make_async_remote_copy(
-            src_ref=rs_mid.at[step, rows, cols],
+        return pltpu.make_async_remote_copy(
+            src_ref=rs_mid.at[step, :, cols],
             dst_ref=rs_two.at[step, k - 1, :, cols],
             send_sem=two_s.at[step, k - 1],
             recv_sem=two_r.at[step, k - 1, j],
@@ -403,55 +422,36 @@
         for k in range(1, NX):
             two_copy(step, k, j).start()
 
-    def x_copy(step, k, j):
-        spot = x_all.at[rows_of(step, core, mx), j * WC : (j + 1) * WC]
+    def pair_copy(step, j):
+        spot = x_all.at[rows_of(step, core, 0, NX), j * WC : (j + 1) * WC]
         return pltpu.make_async_remote_copy(
             src_ref=spot,
             dst_ref=spot,
-            send_sem=x_s.at[step, k - 1],
-            recv_sem=x_r.at[step, k - 1, j],
-            device_id={"col": x_peer(k) * 2 + core},
-            device_id_type=MESH,
-        )
-
-    def pair_copy(step, k, j):
-        spot = x_all.at[rows_of(step, core, x_from(k)), j * WC : (j + 1) * WC]
-        return pltpu.make_async_remote_copy(
-            src_ref=spot,
-            dst_ref=spot,
-            send_sem=pair_s.at[step, k],
+            send_sem=pair_s.at[step],
             recv_sem=pair_r.at[step],
             device_id=partner,
             device_id_type=MESH,
         )
 
     def streams(step):
-        own_rows = rows_of(step, core, mx)
+        rows = rows_of(step, core, 0, NX)
         for j in range(NJ):
             cols = slice(j * WC, (j + 1) * WC)
             value = (
-                resid_rows[own_rows, cols].astype(F32)
-                + proj[own_rows, cols].astype(F32)
-                + rs_one[step, mid_own, cols].astype(F32)
+                resid_rows[rows, cols].astype(F32)
+                + proj[rows, cols].astype(F32)
+                + rs_one[step, :, cols].astype(F32)
             )
             for k in range(1, NX):
                 two_copy(step, k, j).wait_recv()
                 value = value + rs_two[step, k - 1, :, cols].astype(F32)
             stream[step, :, cols] = value
-            x_all[own_rows, cols] = (value * gain[:, cols]).astype(BF16)
-            for k in range(1, NX):
-                x_copy(step, k, j).start()
-            pair_copy(step, 0, j).start()
-
-    def x_forward(step):
-        for j in range(NJ):
-            for k in range(1, NX):
-                x_copy(step, k, j).wait_recv()
-                pair_copy(step, k, j).start()
+            x_all[rows, cols] = (value * gain[:, cols]).astype(BF16)
+            pair_copy(step, j).start()
 
     def x_arrive(step):
         spot = x_all.at[rows_of(step, 1 - core, 0, NX), :]
-        whole(spot, pair_s.at[step, 0], pair_r.at[step]).wait_recv()
+        whole(spot, pair_s.at[step], pair_r.at[step]).wait_recv()
 
     w_copies[0].wait()
     for j in range(NJ + 1):
@@ -462,7 +462,7 @@
 
     @pl.loop(nd // 2, nd)
     def _(k):
-        relay(k)
+        both(k, True)
 
     for k in range(1, nc):
         res_copy(k).wait_recv()
@@ -471,17 +471,28 @@
         resid_rows[:, cols] = lax.dot_general(
             fetch, resid_all[:, cols], (((0,), (0,)), ((), ())), preferred_element_type=F32
         ).astype(BF16)
+
+    is_end = jnp.logical_or(me == 0, me == E)
+
+    def second_part():
+        @pl.loop(nd // 2, nd)
+        def _(k):
+            both(k, False)
+
+        for j in range(NJ):
+            project(1, j)
+
+    @pl.when(jnp.logical_not(is_end))
+    def _():
+        second_part()
+
     streams(0)
 
-    @pl.loop(nd // 2, nd)
-    def _(k):
-        ends(k)
-
-    for j in range(NJ):
-        project(1, j)
-    x_forward(0)
-    for j in range(NJ):
-        meet(1, j)
+    @pl.when(jnp.logical_not(is_end))
+    def _():
+        for j in range(NJ):
+            meet(1, j)
+
     x_arrive(0)
     def neighbour(way):
         return {"dev": me + (1 if way == 0 else -1)}
@@ -585,43 +596,52 @@
     w_copies[1].wait()
     w_copies[2].wait()
 
+    second_start = jnp.where(is_end, END_START, MID_START)
+
     @pl.loop(0, NC + hid_lag(E))
     def _(i):
-        group = i // PHASE
-        turn = halves[0] + group * (halves[1] - halves[0])
+        again = i >= second_start
+        turn = jnp.where(again, halves[1], halves[0])
         turn_rows = pl.ds(pl.multiple_of(turn * half, half), half)
-
-        @pl.when(i == min(LATER, PHASE))
+        place_in = jnp.where(again, i - second_start, i)
+
+        @pl.when(jnp.logical_and(is_end, i == END_PROJ))
+        def _():
+            second_part()
+
+        @pl.when(jnp.logical_and(is_end, i == END_PROJ + 2))
+        def _():
+            for j in range(NJ):
+                meet(1, j)
+
+        @pl.when(i == jnp.where(is_end, END_START - 1, LATER))
         def _():
             streams(1)
 
-        @pl.when(i == min(LATER + 3, PHASE))
-        def _():
-            x_forward(1)
-
-        @pl.when(i == PHASE)
+        @pl.when(i == second_start)
         def _():
             x_arrive(1)
-        for p in range(PACE):
-            q = (i - group * PHASE) * PACE + p
-
-            @pl.when(jnp.logical_and(group < 2, q < NC))
-            def _():
+        @pl.when(place_in < PHASE)
+        def _():
+            value = x_all[turn_rows, :]
+            for p in range(PACE):
+                q = place_in * PACE + p
                 cols = pl.ds(pl.multiple_of(q * CF, CF), CF)
-                value = x_all[turn_rows, :]
                 own[q, turn, :, :CF] = jnp.dot(
                     value, wg[:, cols], preferred_element_type=F32
                 ).astype(BF16)
                 own[q, turn, :, CF:] = jnp.dot(
                     value, wu[:, cols], preferred_element_type=F32
                 ).astype(BF16)
-                for way in (0, 1):
-                    @pl.when(jnp.logical_and(group == 0, me == (0 if way == 0 else E)))
-                    def _():
-                        for r in range(PART):
-                            sum_copy(way, q, r).start()
-
-        @pl.when(jnp.logical_and(group < 2, i == group * PHASE))
+
+        for way in (0, 1):
+            @pl.when(jnp.logical_and(i < PHASE, me == (0 if way == 0 else E)))
+            def _():
+                for p in range(PACE):
+                    for r in range(PART):
+                        sum_copy(way, i * PACE + p, r).start()
+
+        @pl.when(place_in == 0)
         def _():
             squares = jnp.zeros((half, 1), F32)
             for j in range(NJ):
@@ -630,7 +650,7 @@
                 squares = squares + jnp.sum(value * value, axis=1, keepdims=True)
             ss_own[turn_rows, :] = jnp.broadcast_to(squares, (half, ss_own.shape[1]))
             for way in (0, 1):
-                @pl.when(jnp.logical_and(group == 0, me == (0 if way == 0 else E)))
+                @pl.when(jnp.logical_and(i == 0, me == (0 if way == 0 else E)))
                 def _():
                     ssd_copy(way).start()
 
@@ -673,6 +693,7 @@
                     value, jnp.concatenate(right, axis=1), preferred_element_type=F32
                 )
 
+    down = resid_rows
     my_half = pl.ds(pl.multiple_of(core * NX * R, R), NX * R)
     other_half = pl.ds(pl.multiple_of((1 - core) * NX * R, R), NX * R)
 
@@ -701,7 +722,7 @@
 
     for step in (0, 1):
         rows = rows_of(step, core, mx)
-        acc[rows, :] = acc[rows, :] + stream[step]
+        acc[rows, :] = acc[rows, :] + stream[step, mid_own, :]
     for j in range(NJ + 1):
         if j < NJ:
             cols = slice(j * WC, (j + 1) * WC)
@@ -730,25 +751,32 @@
     for k in range(1, nc):
         res_copy(k).wait_send()
     for step in (0, 1):
-        mine = x_all.at[rows_of(step, core, mx), :]
+        mine = x_all.at[rows_of(step, core, 0, NX), :]
         whole(proj.at[rows_of(step, 1 - core, 0, NX), :], one_s.at[step], one_r.at[step, 0]).wait_send()
         for k in range(1, NX):
             whole(mine, two_s.at[step, k - 1], one_r.at[step, 0]).wait_send()
-            whole(mine, x_s.at[step, k - 1], one_r.at[step, 0]).wait_send()
-        for k in range(NX):
-            whole(mine, pair_s.at[step, k], one_r.at[step, 0]).wait_send()
+        whole(mine, pair_s.at[step], one_r.at[step, 0]).wait_send()
     whole(down.at[other_half, :], done_s.at[0], done_r.at[0]).wait_send()
     for k in range(1, NX):
         whole(down.at[my_rows, :], dtwo_s.at[k - 1], done_r.at[0]).wait_send()
 
+    for way in (0, 1):
+        @pl.when(me == (E - 2 if way == 0 else 2))
+        def _():
+            for a in range(2):
+                far_copy(way, a).wait_send()
+
     for a in range(2):
         @pl.loop(0, nd)
         def _(origin):
-            @pl.when(jnp.logical_and(me < E, origin <= me))
+            left = jnp.logical_or(origin == me, jnp.logical_and(origin < me, passes(origin, 0)))
+            right = jnp.logical_or(origin == me, jnp.logical_and(origin > me, passes(origin, 1)))
+
+            @pl.when(jnp.logical_and(me < E, left))
             def _():
                 att_copy(origin, a, 0).wait_send()
 
-            @pl.when(jnp.logical_and(me > 0, origin >= me))
+            @pl.when(jnp.logical_and(me > 0, right))
             def _():
                 att_copy(origin, a, 1).wait_send()
 
@@ -821,9 +849,9 @@
             vmem((T, DK), BF16),
             vmem((2, half // 2, DK), BF16),
             vmem((2, half // 2, DK), BF16),
-            vmem((2, max(NX - 1, 1), half // nc, DK), BF16),
+            vmem((2, max(NX - 1, 1), half // 2, DK), BF16),
             vmem((T, DK), BF16),
-            vmem((2, half // nc, DK), F32),
+            vmem((2, half // 2, DK), F32),
             vmem((NC, 2, half, 2 * CF), BF16),
             vmem((NC, half, 2 * CF), BF16),
             vmem((NC, half, 2 * CF), BF16),
@@ -833,7 +861,6 @@
             vmem((half, 128), F32),
             vmem((NC, T, CF), BF16),
             vmem((T, DK), F32),
-            vmem((T, DK), BF16),
             vmem((NX * R, DK), BF16),
             vmem((NX * R, DK), BF16),
             vmem((max(NX - 1, 1), R, DK), BF16),
@@ -842,15 +869,14 @@
             dma((5,)),
             dma((2, nd, 2)),
             dma((nd, 2)),
+            dma((2, 2)),
             dma((nc - 1,)),
             dma((nc - 1,)),
             dma((2,)),
             dma((2, NJ)),
             dma((2, max(NX - 1, 1))),
             dma((2, max(NX - 1, 1), NJ)),
-            dma((2, max(NX - 1, 1))),
-            dma((2, max(NX - 1, 1), NJ)),
-            dma((2, NX)),
+            dma((2,)),
             dma((2,)),
             dma((2,)),
             dma((2, NC, PART)),
@@ -870,7 +896,7 @@
             out_specs=pl.BlockSpec(memory_space=pltpu.VMEM),
             scratch_shapes=scratch,
             compiler_params=pltpu.CompilerParams(
-                collective_id=0, has_side_effects=True, vmem_limit_bytes=65 * 1000 * 1000
+                collective_id=0, has_side_effects=True, vmem_limit_bytes=67043328 - 2 * R * DK
             ),
         )(
             page_table.T,

time: 74.1 us -> 71.5 us (0.965)
  Pallas kernels: 73.3 us -> 70.7 us
    pallas_call x1, Pallas kernels: 73.3 us -> 70.7 us  [on_device(): pl.pallas_call(functools.partial(layer_kernel, nd, nc, dims), out_shape=p...]
where the time goes in v4:
time: 71.5 us; the launch traced here: 71.4 us
  Pallas kernels  70.7 us (99%)
    pallas_call x1, Pallas kernels, on_device(): pl.pallas_call(functools.partial(layer_kernel, nd, nc, dims), out_shape=p...  70.7 us

profile of v4, /device:TPU:0, one launch (start us, length us, event | category | flops | bytes accessed | tf_op | source)
XLA Modules:
  0.0 71.4 jit_solution(12498994475573850093)
XLA Ops:
  0.0 70.7 %shard_map.109 = bf16[32,2048]{1,0:T(8,128)(2,1)S(1)} custom-call(s32[3,32]{1,0:T(4,128)} %bitcast.8, s32[32]{0:T(128)} %len_hbm.1, bf16[32,2048]{1,0:T(8,128)(2,1)} %q_hbm.1, bf16[192,2,128,128]{3,2,1,0:T(8,128)(2,1)} %bitcast.6, s32[1,128]{1,0:T(1,128)} %bitcast.9, bf16[32,2048]{1,0:T(8,128)(2,1)} %resid_hbm.1, f32[1,2048]{1,0:T(1,128)} %bitcast.7, ...), custom_call_target="tpu_custom_call" | custom-call | tf_op jit(solution)/shard_map/pallas_call | solution.py:892
  70.7 0.7 copy.13

commit v5 on v4

--- a/solution.py
+++ b/solution.py
@@ -19,8 +19,8 @@
 WCM = 1024
 LAG_S0 = 4
 LAG_S = 3
-LAG_H0 = 4
-LAG_H = 5
+LAG_H0 = 3
+LAG_H = 4
 
 
 def divisor(size, choices):

time: 71.5 us -> 71.1 us (level)
  no operation moved by 1% of the time
where the time goes in v5:
time: 71.1 us; the launch traced here: 71 us
  Pallas kernels  70.3 us (99%)
    pallas_call x1, Pallas kernels, on_device(): pl.pallas_call(functools.partial(layer_kernel, nd, nc, dims), out_shape=p...  70.3 us

profile of v5, /device:TPU:0, one launch (start us, length us, event | category | flops | bytes accessed | tf_op | source)
XLA Modules:
  0.0 71.0 jit_solution(3999287252191123087)
XLA Ops:
  0.0 70.3 %shard_map.109 = bf16[32,2048]{1,0:T(8,128)(2,1)S(1)} custom-call(s32[3,32]{1,0:T(4,128)} %bitcast.8, s32[32]{0:T(128)} %len_hbm.1, bf16[32,2048]{1,0:T(8,128)(2,1)} %q_hbm.1, bf16[192,2,128,128]{3,2,1,0:T(8,128)(2,1)} %bitcast.6, s32[1,128]{1,0:T(1,128)} %bitcast.9, bf16[32,2048]{1,0:T(8,128)(2,1)} %resid_hbm.1, f32[1,2048]{1,0:T(1,128)} %bitcast.7, ...), custom_call_target="tpu_custom_call" | custom-call | tf_op jit(solution)/shard_map/pallas_call | solution.py:892
  70.3 0.7 copy.13
